TPU v7x, 32 devices: a whole 2x2x4 slice. The times are simulated.
32 devices in a mesh: dp: 2 (over x), tp: 4 (over z), sp: 4 (over y, core).
Axes of the slice: x: 2, y: 2, z: 4, core: 2. Of those that a mesh axis runs over, the one named last changes fastest.
Arguments:
- x_in: bfloat16 [32, 4096, 1024], P('dp', ('tp', 'sp')), parts along dimension 0
- q_out: bfloat16 [32, 4096, 1024], P('dp', ('tp', 'sp')), parts along dimension 0
- latents: bfloat16 [64, 1024], replicated
- norm_in: float32 [2, 1024], replicated
- norm_query: float32 [2, 1024], replicated
- norm_lat: float32 [8, 2, 1024], replicated
- enc_wq: bfloat16 [1024, 1024], replicated
- enc_wkv: bfloat16 [2, 1024, 1024], replicated
- enc_wo: bfloat16 [1024, 1024], replicated
- enc_mlp: bfloat16 [2, 1024, 1024], replicated
- lat_wqkv: bfloat16 [2, 1024, 3, 8, 128], P(None, None, None, 'tp')
- lat_wo: bfloat16 [2, 8, 128, 1024], P(None, 'tp')
- lat_w1: bfloat16 [2, 1024, 4096], P(None, None, 'tp')
- lat_w2: bfloat16 [2, 4096, 1024], P(None, 'tp')
- dec_wq: bfloat16 [1024, 1024], replicated
- dec_wkv: bfloat16 [2, 1024, 1024], replicated
- dec_wo: bfloat16 [1024, 1024], replicated
- dec_mlp: bfloat16 [2, 1024, 1024], replicated
- dec_out: bfloat16 [1024, 1024], replicated
Outputs:
- output: float32 [32, 4096, 1024], P('dp', ('tp', 'sp')), parts along dimension 0
There are 2 independent parts. A program takes and returns all parts, laid end to end along the dimension named above; an argument that names none is the same for every part.
All inputs are finite; a program needn't handle non-finite values.
Results may differ from a plain program's by a relative error of at most 0.0104939.
Values sent between devices are 32-bit elements.
A program may use at most 1 GiB of HBM per device.

v0:
```python
import math
import jax
import jax.numpy as jnp
from jax import lax
from jax.sharding import PartitionSpec as P

LN_EPS = 1e-5
GROUP_AXES = ('tp', 'sp')


def layer_norm(values, params):
    val_f32 = values.astype(jnp.float32)
    row_mean = jnp.mean(val_f32, axis=-1, keepdims=True)
    centered = val_f32 - row_mean
    row_var = jnp.mean(centered * centered, axis=-1, keepdims=True)
    return (centered * lax.rsqrt(row_var + LN_EPS) * params[0] + params[1]).astype(jnp.bfloat16)


def mlp_part(residual, norm_params, w_up, w_down):
    hidden = jax.nn.gelu(jnp.einsum('bne,ef->bnf', layer_norm(residual, norm_params), w_up, preferred_element_type=jnp.float32))
    return jnp.einsum('bnf,fe->bne', hidden.astype(jnp.bfloat16), w_down, preferred_element_type=jnp.float32)


def attention_part(latent, norm_params, w_qkv, w_out):
    head_dim = w_qkv.shape[3]
    qkv_proj = jnp.einsum('bne,ethf->tbnhf', layer_norm(latent, norm_params), w_qkv, preferred_element_type=jnp.float32).astype(jnp.bfloat16)
    att_scores = jnp.einsum('bnhf,bmhf->bhnm', qkv_proj[0], qkv_proj[1], preferred_element_type=jnp.float32) / math.sqrt(head_dim)
    att_probs = jax.nn.softmax(att_scores, axis=-1).astype(jnp.bfloat16)
    att_out = jnp.einsum('bhnm,bmhf->bnhf', att_probs, qkv_proj[2], preferred_element_type=jnp.float32).astype(jnp.bfloat16)
    return jnp.einsum('bnhf,hfe->bne', att_out, w_out, preferred_element_type=jnp.float32)


def decoder(latent, q_loc, norm_query, norm_lat, dec_wq, dec_wkv, dec_wo, dec_mlp, dec_out):
    model_dim = latent.shape[2]
    normed_z = layer_norm(latent, norm_lat[6])
    key_dec = jnp.einsum('bne,ef->bnf', normed_z, dec_wkv[0], preferred_element_type=jnp.float32).astype(jnp.bfloat16)
    val_dec = jnp.einsum('bne,ef->bnf', normed_z, dec_wkv[1], preferred_element_type=jnp.float32).astype(jnp.bfloat16)
    query_dec = jnp.einsum('bpc,ce->bpe', layer_norm(q_loc, norm_query), dec_wq, preferred_element_type=jnp.float32).astype(jnp.bfloat16)
    dec_scores = jnp.einsum('bpe,bne->bpn', query_dec, key_dec, preferred_element_type=jnp.float32) / math.sqrt(model_dim)
    dec_probs = jax.nn.softmax(dec_scores, axis=-1).astype(jnp.bfloat16)
    attended = jnp.einsum('bpn,bne->bpe', dec_probs, val_dec, preferred_element_type=jnp.float32).astype(jnp.bfloat16)
    output = jnp.einsum('bpe,ef->bpf', attended, dec_wo, preferred_element_type=jnp.float32)
    output = output + mlp_part(output, norm_lat[7], dec_mlp[0], dec_mlp[1])
    return jnp.einsum('bpe,eo->bpo', output.astype(jnp.bfloat16), dec_out, preferred_element_type=jnp.float32)


def solution(mesh):
    seq_spec = P('dp', ('tp', 'sp'), None)
    replicated = P()
    in_specs = (seq_spec, seq_spec, replicated, replicated, replicated, replicated, replicated, replicated, replicated, replicated,
                P(None, None, None, 'tp', None), P(None, 'tp', None, None), P(None, None, 'tp'), P(None, 'tp', None),
                replicated, replicated, replicated, replicated, replicated)

    def device_step(x_loc, q_loc, latents, norm_in, norm_query, norm_lat, enc_wq, enc_wkv, enc_wo, enc_mlp,
                    lat_wqkv, lat_wo, lat_w1, lat_w2, dec_wq, dec_wkv, dec_wo, dec_mlp, dec_out):
        model_dim = latents.shape[1]
        query_enc = jnp.dot(layer_norm(latents, norm_lat[0]), enc_wq, preferred_element_type=jnp.float32).astype(jnp.bfloat16)
        normed_x = layer_norm(x_loc, norm_in)
        key_enc = jnp.einsum('bpc,ce->bpe', normed_x, enc_wkv[0], preferred_element_type=jnp.float32).astype(jnp.bfloat16)
        val_enc = jnp.einsum('bpc,ce->bpe', normed_x, enc_wkv[1], preferred_element_type=jnp.float32).astype(jnp.bfloat16)
        scores = jnp.einsum('ne,bpe->bnp', query_enc, key_enc, preferred_element_type=jnp.float32) / math.sqrt(model_dim)
        row_max = lax.pmax(jnp.max(scores, axis=2, keepdims=True), GROUP_AXES)
        weights = jnp.exp(scores - row_max)
        local_num = jnp.einsum('bnp,bpe->bne', weights.astype(jnp.bfloat16), val_enc, preferred_element_type=jnp.float32)
        numerator, denominator = lax.psum((local_num, jnp.sum(weights, axis=2, keepdims=True)), GROUP_AXES)
        attended = (numerator / denominator).astype(jnp.bfloat16)
        latent = latents.astype(jnp.float32)[None] + jnp.einsum('bne,ef->bnf', attended, enc_wo, preferred_element_type=jnp.float32)
        latent = latent + mlp_part(latent, norm_lat[1], enc_mlp[0], enc_mlp[1])
        for layer_index in range(lat_wqkv.shape[0]):
            att_sum = attention_part(latent, norm_lat[2 + 2 * layer_index], lat_wqkv[layer_index], lat_wo[layer_index])
            latent = latent + lax.psum(att_sum, 'tp')
            mlp_sum = mlp_part(latent, norm_lat[3 + 2 * layer_index], lat_w1[layer_index], lat_w2[layer_index])
            latent = latent + lax.psum(mlp_sum, 'tp')
        return decoder(latent, q_loc, norm_query, norm_lat, dec_wq, dec_wkv, dec_wo, dec_mlp, dec_out)

    return jax.shard_map(device_step, mesh=mesh, in_specs=in_specs, out_specs=seq_spec, check_vma=False)
```

profile of v0, /device:TPU:0, one launch (start us, length us, event | category | flops | bytes accessed | tf_op | source)
XLA Modules:
  0.0 993.6 jit_solution(5320637054497871754)
XLA Ops:
  6.5 1.2 convert_reduce_fusion.2
  7.7 1.1 multiply_reduce_fusion.7
  8.8 0.8 fusion.291
  9.7 4.7 convert_reduce_fusion
  14.4 1.0 copy-done.4
  15.4 2.8 fusion.7
  18.3 0.7 fusion.289
  19.0 0.5 fusion.241
  19.5 15.6 %fusion.292 = (f32[16,64]{1,0:T(8,128)S(1)}, f32[16,64,256]{2,1,0:T(8,128)S(1)}) fusion(bf16[64,1024,1]{1,0,2:T(8,128)(2,1)S(1)} %fusion.241, bf16[16,256,1024]{2,1,0:T(8,128)(2,1)} %param.19, f32[1024]{0:T(1024)S(1)} %bitcast.239, f32[1024]{0:T(1024)S(1)} %bitcast.237, f32[16,256]{1,0:T(8,128)S(1)} %add_rsqrt_fusion.1, ...), kind=kOutput, calls=%fused_computation.276 | convolution fusion | flops 9156688896 | bytes 11710464 | tf_op jit(solution)/shard_map/ne,bpe->bnp/dot_general | solution.py:61
  35.1 35.7 %pmax.7 = f32[16,64]{1,0:T(8,128)S(1)} all-reduce(f32[16,64]{1,0:T(8,128)S(1)} %get-tuple-element.35), channel_id=1, replica_groups=mesh['dp'=2,'tp'=4,'sp'=4] {'tp','sp'}, use_global_device_ids=true, to_apply=%region_7.0 | all-reduce | flops 1024 | bytes 8192 | tf_op jit(solution)/shard_map/pmax | solution.py:62
  70.8 15.8 %fusion.39 = f32[16,64,1024]{2,1,0:T(8,128)} fusion(bf16[16,256,1024]{2,1,0:T(8,128)(2,1)} %param.19, f32[1024]{0:T(1024)S(1)} %bitcast.240, f32[1024]{0:T(1024)S(1)} %bitcast.238, f32[16,256]{1,0:T(8,128)S(1)} %add_rsqrt_fusion.1, f32[16,256]{1,0:T(8,128)S(1)} %broadcast_multiply_fusion.1, bf16[2,1024,1024]{2,1,0:T(8,128)(2,1)} %param.26, ...), kind=kOutput, calls=%fused_computation.42 | convolution fusion | flops 9156689920 | bytes 15773696 | tf_op jit(solution)/shard_map/bnp,bpe->bne/dot_general | solution.py:64
  86.5 0.0 all-reduce.6.cloned.1.call-update
  86.6 0.0 all-reduce.8.cloned.1.call-start
  86.7 0.4 fusion.242
  87.1 31.6 %psum.43 = f32[16,64]{1,0:T(8,128)S(1)} all-reduce(f32[16,64]{1,0:T(8,128)S(1)} %fusion.242), channel_id=1, replica_groups=mesh['dp'=2,'tp'=4,'sp'=4] {'tp','sp'}, use_global_device_ids=true, to_apply=%region_10.0 | all-reduce | flops 1024 | bytes 8192 | tf_op jit(solution)/shard_map/psum | solution.py:65
  118.6 5.4 fusion.288
  124.1 71.5 %all-reduce.6.cloned.1.call-done = f32[16,64,1024]{2,1,0:T(8,128)} async-done(((f32[16,64,1024]{2,1,0:T(8,128)}), f32[16,64,1024]{2,1,0:T(8,128)}) %all-reduce.6.cloned.1.call-update) | async-done | bytes 4194320 | tf_op jit(solution)/shard_map/psum | solution.py:65
  195.6 5.4 add_reduce_fusion
  201.0 2.0 copy-done.6
  203.0 0.8 multiply_reduce_fusion.6
  203.8 9.8 fusion.297
  213.6 2.9 multiply_reduce_fusion.5
  216.5 0.5 copy-done.5
  217.0 4.7 fusion.199
  221.7 1.7 fusion.300
  223.4 1.6 convolution_multiply_fusion.1
  225.0 4.3 convolution_bitcast_fusion.1
  229.3 0.5 all-reduce.10.cloned.1.call-start
  229.8 152.5 %all-reduce.8.cloned.1.call-done = f32[16,64,1024]{2,1,0:T(8,128)} async-done(((f32[16,64,1024]{2,1,0:T(8,128)}), f32[16,64,1024]{2,1,0:T(8,128)}) %all-reduce.8.cloned.1.call-update) | async-done | bytes 4194320 | tf_op jit(solution)/shard_map/psum | solution.py:71
  382.3 4.0 fusion.287
  386.3 2.0 copy-done.3
  388.3 0.6 multiply_reduce_fusion.4
  388.9 10.1 %fusion.103 = f32[16,64,1024]{2,1,0:T(8,128)} fusion(bf16[2,1024,1024]{2,1,0:T(8,128)(2,1)} %param.32, f32[16,64,1024]{2,1,0:T(8,128)} %copy-done.3, bf16[2,1024,1024]{2,1,0:T(8,128)(2,1)} %param.31, f32[1024]{0:T(1024)S(1)} %bitcast.231, f32[1024]{0:T(1024)S(1)} %bitcast.232, f32[16,64]{1,0:T(8,128)S(1)} %add_rsqrt_fusion.6, ...), kind=kOutput, calls=%fused_computation.108 | convolution fusion | flops 4309647360 | bytes 12599296 | tf_op jit(solution)/shard_map/bnf,fe->bne/dot_general | solution.py:21
  399.0 0.0 all-reduce.12.cloned.1.call-start
  399.1 153.0 %all-reduce.10.cloned.1.call-done = f32[16,64,1024]{2,1,0:T(8,128)} async-done(((f32[16,64,1024]{2,1,0:T(8,128)}), f32[16,64,1024]{2,1,0:T(8,128)}) %all-reduce.10.cloned.1.call-update) | async-done | bytes 4194320 | tf_op jit(solution)/shard_map/psum | solution.py:73
  552.1 4.0 fusion.286
  556.1 0.6 multiply_reduce_fusion.3
  556.7 1.4 copy-done.1
  558.1 0.6 copy-done.9
  558.6 3.3 fusion.202
  561.9 1.7 fusion.301
  563.6 1.6 convolution_multiply_fusion
  565.2 4.2 convolution_bitcast_fusion
  569.4 0.2 all-reduce.14.cloned.1.call-start
  569.6 152.8 %all-reduce.12.cloned.1.call-done = f32[16,64,1024]{2,1,0:T(8,128)} async-done(((f32[16,64,1024]{2,1,0:T(8,128)}), f32[16,64,1024]{2,1,0:T(8,128)}) %all-reduce.12.cloned.1.call-update) | async-done | bytes 4194320 | tf_op jit(solution)/shard_map/psum | solution.py:71
  722.5 4.0 fusion.285
  726.5 2.0 copy-done.2
  728.4 0.6 multiply_reduce_fusion.2
  729.0 10.1 %fusion.101 = f32[16,64,1024]{2,1,0:T(8,128)} fusion(bf16[2,1024,1024]{2,1,0:T(8,128)(2,1)} %param.32, f32[16,64,1024]{2,1,0:T(8,128)} %copy-done.2, bf16[2,1024,1024]{2,1,0:T(8,128)(2,1)} %param.31, f32[1024]{0:T(1024)S(1)} %bitcast.227, f32[1024]{0:T(1024)S(1)} %bitcast.228, f32[16,64]{1,0:T(8,128)S(1)} %add_rsqrt_fusion.4, ...), kind=kOutput, calls=%fused_computation.107 | convolution fusion | flops 4309647360 | bytes 12599296 | tf_op jit(solution)/shard_map/bnf,fe->bne/dot_general | solution.py:21
  739.1 0.7 copy-done.11
  739.8 4.5 convert_reduce_fusion.1
  744.4 5.7 fusion.11
  750.1 142.1 %all-reduce.14.cloned.1.call-done = f32[16,64,1024]{2,1,0:T(8,128)} async-done(((f32[16,64,1024]{2,1,0:T(8,128)}), f32[16,64,1024]{2,1,0:T(8,128)}) %all-reduce.14.cloned.1.call-update) | async-done | bytes 4194320 | tf_op jit(solution)/shard_map/psum | solution.py:73
  892.2 4.0 fusion.284
  896.2 0.6 multiply_reduce_fusion.1
  896.8 1.6 copy-done.24
  898.4 3.8 fusion.113
  902.2 3.8 fusion.115
  905.9 15.8 %fusion.205 = f32[16,256,64]{1,2,0:T(8,128)S(1)} fusion(bf16[16,64,1024]{2,1,0:T(8,128)(2,1)} %fusion.115, bf16[16,256,1024]{2,1,0:T(8,128)(2,1)} %param.20, f32[1024]{0:T(1024)S(1)} %bitcast.242, f32[1024]{0:T(1024)S(1)} %bitcast.241, f32[16,256]{1,0:T(8,128)S(1)} %add_rsqrt_fusion.2, f32[16,256]{1,0:T(8,128)S(1)} %broadcast_multiply_fusion.2, ...), kind=kOutput, calls=%fused_computation.186 | convolution fusion | flops 9156427776 | bytes 13672448 | tf_op jit(solution)/shard_map/bpe,bne->bpn/dot_general | solution.py:39
  921.8 0.2 fusion.302
  922.0 16.3 %fusion.303 = (f32[16,256]{1,0:T(8,128)S(1)}, f32[16,256,1024]{2,1,0:T(8,128)}) fusion(bf16[1024,1024]{1,0:T(8,128)(2,1)S(1)} %copy-done, bf16[16,64,1024]{2,1,0:T(8,128)(2,1)} %fusion.113, f32[16,256]{1,0:T(8,128)S(1)} %fusion.302, f32[16,256,64]{1,2,0:T(8,128)S(1)} %fusion.205), kind=kOutput, calls=%fused_computation.281 | convolution fusion | flops 9135980544 | bytes 22052864 | tf_op jit(solution)/shard_map/bpe,ef->bpf/dot_general | solution.py:42
  938.4 7.0 multiply_reduce_fusion
  945.5 24.6 %add_convert_fusion = bf16[16,256,1024]{2,1,0:T(8,128)(2,1)} fusion(f32[16,256,1024]{2,1,0:T(8,128)} %get-tuple-element.42, f32[1024]{0:T(1024)S(1)} %bitcast.222, f32[1024]{0:T(1024)S(1)} %bitcast.221, f32[16,256]{1,0:T(8,128)S(1)} %add_rsqrt_fusion, f32[16,256]{1,0:T(8,128)S(1)} %broadcast_multiply_fusion, bf16[2,1024,1024]{2,1,0:T(8,128)(2,1)} %param.36), kind=kOutput, calls=%fused_computation.28 | convolution fusion | flops 17246978048 | bytes 46178304 | tf_op jit(solution)/shard_map/bnf,fe->bne/dot_general | solution.py:21
  970.0 16.5 %fusion.107 = f32[16,256,1024]{2,1,0:T(8,128)} fusion(bf16[16,256,1024]{2,1,0:T(8,128)(2,1)} %add_convert_fusion, bf16[1024,1024]{1,0:T(8,128)(2,1)} %param.37), kind=kOutput, calls=%fused_computation.110 | convolution fusion | flops 8589934592 | bytes 27262976 | tf_op jit(solution)/shard_map/bpe,eo->bpo/dot_general | solution.py:44
  (68 shorter events, 0.3 us)
Async XLA Ops:
  6.5 915.5 %copy-start = (bf16[1024,1024]{1,0:T(8,128)(2,1)S(1)}, bf16[1024,1024]{1,0:T(8,128)(2,1)}, u32[]{:S(2)}) copy-start(bf16[1024,1024]{1,0:T(8,128)(2,1)} %param.35) | copy-start | bytes 6291460
  6.5 189.0 %all-reduce.6.cloned.1.call-start = ((), (), s32[]{:S(2)}) async-start(), calls=%async_computation | async-start | bytes 8388608 | tf_op jit(solution)/shard_map/psum | solution.py:65
  9.6 5.8 copy-start.4
  15.4 2.9 copy-start.10
  15.4 3.5 copy-start.7
  15.4 3.5 copy-start.8
  86.6 295.8 %all-reduce.8.cloned.1.call-start = ((), (), s32[]{:S(2)}) async-start(), calls=%async_computation.1 | async-start | bytes 8388608 | tf_op jit(solution)/shard_map/psum | solution.py:71
  200.9 2.0 copy-start.6
  201.0 2.8 copy-start.22
  201.0 2.8 copy-start.23
  213.5 3.4 copy-start.5
  213.5 3.4 copy-start.20
  213.5 3.5 copy-start.21
  229.3 322.8 %all-reduce.10.cloned.1.call-start = ((), (), s32[]{:S(2)}) async-start(), calls=%async_computation.2 | async-start | bytes 8388608 | tf_op jit(solution)/shard_map/psum | solution.py:73
  386.3 2.0 copy-start.3
  386.3 2.6 copy-start.18
  386.3 2.6 copy-start.19
  399.0 323.5 %all-reduce.12.cloned.1.call-start = ((), (), s32[]{:S(2)}) async-start(), calls=%async_computation.3 | async-start | bytes 8388608 | tf_op jit(solution)/shard_map/psum | solution.py:71
  556.0 2.0 copy-start.1
  556.0 2.6 copy-start.9
  556.1 2.6 copy-start.16
  556.1 2.6 copy-start.17
  569.4 322.8 %all-reduce.14.cloned.1.call-start = ((), (), s32[]{:S(2)}) async-start(), calls=%async_computation.4 | async-start | bytes 8388608 | tf_op jit(solution)/shard_map/psum | solution.py:73
  726.4 2.0 copy-start.2
  726.4 2.6 copy-start.14
  726.4 2.6 copy-start.15
  739.1 0.7 copy-start.11
  896.2 2.2 copy-start.24
  938.4 7.1 copy-start.12
  938.4 7.1 copy-start.13
Sparse Core Ops, SparseCore 0:
  86.7 108.8 all-reduce.5
  229.4 152.8 all-reduce.7
  399.1 152.9 all-reduce.9
  569.5 152.8 all-reduce.11
  739.2 152.9 all-reduce.13
where the time goes:
time: 1000 us; the launch traced here: 994 us
  waiting for transfers between devices  672 us (67%)
  matrix products  171 us (17%)
  blocking collectives  67.3 us (7%)
  other arithmetic  49.6 us (5%)
  local copies, waits for them, and re-layouts  18.7 us (2%)
  between operations  14.2 us (1%)
    psum x2, waiting for transfers between devices, device_step(): latent = latent + lax.psum(att_sum, 'tp')  305 us
    psum x2, waiting for transfers between devices, device_step(): latent = latent + lax.psum(mlp_sum, 'tp')  295 us
    psum x1, waiting for transfers between devices, device_step(): lax.psum((local_num, jnp.sum(weights, axis=2, keepdims=True)), GROUP_AXES)  71.5 us
    dot_general x4, matrix products, mlp_part(): jnp.einsum('bnf,fe->bne', hidden.astype(jnp.bfloat16), w_down, preferred_...  54.5 us
    pmax x1, blocking collectives, device_step(): row_max = lax.pmax(jnp.max(scores, axis=2, keepdims=True), GROUP_AXES)  35.7 us
    psum x1, blocking collectives, device_step(): lax.psum((local_num, jnp.sum(weights, axis=2, keepdims=True)), GROUP_AXES)  31.6 us
    reduce_sum x7, other arithmetic, layer_norm(): row_mean = jnp.mean(val_f32, axis=-1, keepdims=True)  26.3 us
    reduce_sum x10, other arithmetic, layer_norm(): row_var = jnp.mean(centered * centered, axis=-1, keepdims=True)  22.5 us
  transfers between devices with their start and end apart: 5, of which 5 were waited for; matrix products, arithmetic and copies ran while one was open for 2% of the time, Pallas kernels for 0%

commit v1 on v0

v1 whole, which is shorter than its diff:
```python
import functools
import math
import jax
import jax.numpy as jnp
from jax import lax
from jax.experimental import pallas as pl
from jax.experimental.pallas import tpu as pltpu
from jax.sharding import PartitionSpec as P

LN_EPS = 1e-5
F32, BF16 = jnp.float32, jnp.bfloat16
MESH = pl.DeviceIdType.MESH
VMEM_LIMIT = 60 * 1024 * 1024
LANES = 128
NLINE = 4
NCH = 4
GELU_C = math.sqrt(2.0 / math.pi)


def layer_norm(values, gain, bias):
    row_mean = jnp.mean(values, axis=-1, keepdims=True)
    centered = values - row_mean
    row_var = jnp.mean(centered * centered, axis=-1, keepdims=True)
    return (centered * lax.rsqrt(row_var + LN_EPS) * gain + bias).astype(BF16)


def gelu(x):
    return 0.5 * x * (1.0 + jnp.tanh(GELU_C * (x + 0.044715 * (x * x * x))))


def dot(a, b):
    return jnp.dot(a, b, preferred_element_type=F32)


def dot_t(a, b):
    return lax.dot_general(a, b, (((1,), (1,)), ((), ())), preferred_element_type=F32)


def split_bf16(x):
    high = x.astype(BF16)
    return high, (x - high.astype(F32)).astype(BF16)


def encoder_kernel(x_ref, nin_ref, lat_ref, nq_ref, wq_ref, wk_ref, num_ref, st_ref, qk_s, stats_s):
    b = pl.program_id(0)
    n = lat_ref.shape[0]
    dim = lat_ref.shape[1]

    @pl.when(b == 0)
    def _():
        q = dot(layer_norm(lat_ref[...].astype(F32), nq_ref[0:1, :], nq_ref[1:2, :]), wq_ref[...]).astype(BF16)
        high, low = split_bf16(dot_t(q, wk_ref[0]))
        qk_s[0:n, :] = high
        qk_s[n:2 * n, :] = low
        stats_s[...] = jnp.zeros_like(stats_s)

    xn = layer_norm(x_ref[0].astype(F32), nin_ref[0:1, :], nin_ref[1:2, :])
    both = dot_t(qk_s[...], xn)
    scores = (both[:n] + both[n:]) * (1.0 / math.sqrt(dim))
    row_max = jnp.max(scores, axis=1, keepdims=True)
    weights = jnp.exp(scores - row_max)
    row_sum = jnp.sum(weights, axis=1, keepdims=True)
    num_ref[0] = dot(weights.astype(BF16), xn)
    here = lax.broadcasted_iota(jnp.int32, (n, LANES), 1) == b
    stats_s[0:n, :] = jnp.where(here, row_max, stats_s[0:n, :])
    stats_s[n:2 * n, :] = jnp.where(here, row_sum, stats_s[n:2 * n, :])

    @pl.when(b == pl.num_programs(0) - 1)
    def _():
        st_ref[...] = stats_s[...].T[0:st_ref.shape[0], :]


def encoder_local(x_loc, norm_in, latents, norm_q, enc_wq, enc_wkv):
    nb, rows, dim = x_loc.shape
    n = latents.shape[0]
    whole = lambda shape: pl.BlockSpec(shape, lambda b: (0,) * len(shape))
    return pl.pallas_call(
        encoder_kernel,
        grid=(nb,),
        in_specs=[pl.BlockSpec((1, rows, dim), lambda b: (b, 0, 0)), whole((2, dim)), whole((n, dim)), whole((2, dim)),
                  whole((dim, dim)), pl.BlockSpec((1, dim, dim), lambda b: (0, 0, 0))],
        out_specs=[pl.BlockSpec((1, n, dim), lambda b: (b, 0, 0)), whole((nb, LANES))],
        out_shape=[jax.ShapeDtypeStruct((nb, n, dim), F32), jax.ShapeDtypeStruct((nb, LANES), F32)],
        scratch_shapes=[pltpu.VMEM((2 * n, dim), BF16), pltpu.VMEM((LANES, LANES), F32)],
        compiler_params=pltpu.CompilerParams(vmem_limit_bytes=VMEM_LIMIT),
        name='enc_local',
    )(x_loc, norm_in, latents, norm_q, enc_wq, enc_wkv)


def latent_kernel(num_ref, st_ref, lat_ref, nlat_ref, wkv_h, wo_h, emlp_h, qkv_h, lwo_h, lw1_h, lw2_h, out_ref,
                  wv, wo, emlp, wqkv, lwo, lw1, lw2, wsem,
                  st_all, gs, d2d, ysend, yrecv, zsum, rz_a, rz_b, ln_n, ln_f, ac_n, ac_f, zown, zall,
                  s_st, r_st, s_d2, r_d2, s_y, r_y, s_za, s_zb, r_za, r_zb,
                  s_lnn, s_lnf, s_acn, s_acf, r_lnn, r_lnf, r_acn, r_acf, r_ag, s_agz, s_agc, s_agy):
    n, dim = lat_ref.shape
    rows = n // NCH
    x = lax.axis_index('dp')
    t = lax.axis_index('tp')
    sp = lax.axis_index('sp')
    y = lax.div(sp, 2)
    c = lax.rem(sp, 2)
    me = t * 4 + sp
    upper = lax.div(t, 2)
    is_end = jnp.logical_or(t == 0, t == NLINE - 1)
    is_mid = jnp.logical_not(is_end)
    e_near = upper
    e_far = 1 - upper
    inward = (x, jnp.where(t == 0, 1, jnp.where(t == 1, 2, jnp.where(t == 2, 1, 2))), sp)
    outward = (x, jnp.where(t <= 1, 0, NLINE - 1), sp)
    core_peer = (x, t, y * 2 + (1 - c))
    y_peer = (x, t, (1 - y) * 2 + c)

    def rc(src, dst, ssem, rsem, dev):
        return pltpu.make_async_remote_copy(src_ref=src, dst_ref=dst, send_sem=ssem, recv_sem=rsem,
                                            device_id=dev, device_id_type=MESH)

    def peer(p):
        g = lax.rem(me + p, 16)
        return g, (x, lax.div(g, 4), lax.rem(g, 4))

    loads = [pltpu.make_async_copy(src, dst, wsem.at[i]) for i, (src, dst) in enumerate(
        ((wkv_h.at[1], wv), (wo_h, wo), (emlp_h, emlp), (qkv_h, wqkv), (lwo_h, lwo), (lw1_h, lw1), (lw2_h, lw2)))]
    for load in loads:
        load.start()

    barrier = pltpu.get_barrier_semaphore()

    def greet(p, carry):
        pl.semaphore_signal(barrier, inc=1, device_id=peer(p)[1], device_id_type=MESH)
        return carry

    lax.fori_loop(1, 16, greet, 0)
    pl.semaphore_wait(barrier, 15)

    def send_stats(p, carry):
        g, dev = peer(p)
        rc(st_ref, st_all.at[me], s_st.at[g], r_st.at[me], dev).start()
        return carry

    lax.fori_loop(1, 16, send_stats, 0)

    def core_copy(i, yb):
        return rc(num_ref.at[pl.ds(yb * 8 + (1 - c) * 4 + i * 2, 2)], d2d.at[i, yb], s_d2.at[i, yb], r_d2.at[i, yb], core_peer)

    for i in range(2):
        core_copy(i, 1 - y).start()
        core_copy(i, y).start()
    st_all[me] = st_ref[...]

    def wait_stats(p, carry):
        g, dev = peer(p)
        rc(st_ref, st_all.at[g], s_st.at[g], r_st.at[g], dev).wait_recv()
        return carry

    lax.fori_loop(1, 16, wait_stats, 0)
    top = lax.fori_loop(1, 16, lambda d, m: jnp.maximum(m, st_all[d]), st_all[0])

    def add_sum(d, total):
        stats = st_all[d]
        return total + jnp.exp(stats - top) * pltpu.roll(stats, n, 1)

    total = lax.fori_loop(0, 16, add_sum, jnp.zeros_like(top))
    partner = t * 4 + y * 2 + (1 - c)
    gs[...] = jnp.zeros_like(gs)
    gs[0:16, :] = jnp.exp(st_all[me] - top) / total
    scale_own = gs[...].T[0:n, :]
    gs[0:16, :] = jnp.exp(st_all[partner] - top) / total
    scale_peer = gs[...].T[0:n, :]
    gs[0:n, :] = scale_own
    gs[n:2 * n, :] = scale_peer
    lane = lax.broadcasted_iota(jnp.int32, (2 * n, LANES), 1)

    def y_copy(i, e):
        return rc(ysend.at[i, e], yrecv.at[i, e], s_y.at[i, e], r_y.at[i, e], y_peer)

    def scaled(i, yb, e):
        b = yb * 8 + c * 4 + i * 2 + e
        col = jnp.sum(jnp.where(lane == b, gs[...], 0.0), axis=1, keepdims=True)
        return col[0:n] * num_ref[b] + col[n:2 * n] * d2d[i, yb, e]

    def scale_step(i, carry):
        core_copy(i, 1 - y).wait_recv()
        for e in range(2):
            ysend[i, e] = scaled(i, 1 - y, e)
            y_copy(i, e).start()
        core_copy(i, y).wait_recv()
        for e in range(2):
            zsum[i, e] = scaled(i, y, e)
        return carry

    lax.fori_loop(0, 2, scale_step, 0)

    def y_add(i):
        for e in range(2):
            y_copy(i, e).wait_recv()
            zsum[i, e] = zsum[i, e] + yrecv[i, e]

    def chunk(ch):
        return pl.ds(pl.multiple_of(ch * rows, rows), rows)

    def z_end_send(i):
        def step(ch, carry):
            rc(zsum.at[i, e_far, chunk(ch)], rz_a.at[i, chunk(ch)], s_za.at[i, ch], r_za.at[i, ch], inward).start()
            return carry
        lax.fori_loop(0, NCH, step, 0)

    def z_mid(i):
        def near(ch, carry):
            cp = rc(rz_a.at[i, chunk(ch)], rz_b.at[i, chunk(ch)], s_za.at[i, ch], r_zb.at[i, ch], inward)
            rc(rz_a.at[i, chunk(ch)], rz_a.at[i, chunk(ch)], s_za.at[i, ch], r_za.at[i, ch], outward).wait_recv()
            rz_a[i, chunk(ch)] = rz_a[i, chunk(ch)] + zsum[i, e_far, chunk(ch)]
            cp.start()
            return carry

        def far(ch, carry):
            cp = rc(rz_b.at[i, chunk(ch)], rz_b.at[i, chunk(ch)], s_zb.at[i, ch], r_zb.at[i, ch], outward)
            cp.wait_recv()
            rz_b[i, chunk(ch)] = rz_b[i, chunk(ch)] + zsum[i, e_near, chunk(ch)]
            cp.start()
            return carry

        lax.fori_loop(0, NCH, near, 0)
        lax.fori_loop(0, NCH, far, 0)

    def z_end_recv(i):
        def step(ch, carry):
            rc(rz_b.at[i, chunk(ch)], rz_b.at[i, chunk(ch)], s_zb.at[i, ch], r_zb.at[i, ch], inward).wait_recv()
            return carry
        lax.fori_loop(0, NCH, step, 0)
        return rz_b[i] + zsum[i, e_near]

    def norm(index, values):
        return layer_norm(values, nlat_ref[index, 0:1, :], nlat_ref[index, 1:2, :])

    def attention(layer, xn):
        hd = wqkv.shape[2] // 6
        qkv = dot(xn, wqkv[layer]).astype(BF16)
        outs = []
        for h in range(2):
            q, k, v = (qkv[:, (2 * j + h) * hd:(2 * j + h + 1) * hd] for j in range(3))
            scores = dot_t(q, k) * (1.0 / math.sqrt(hd))
            weights = jnp.exp(scores - jnp.max(scores, axis=1, keepdims=True))
            probs = (weights / jnp.sum(weights, axis=1, keepdims=True)).astype(BF16)
            outs.append(dot(probs, v).astype(BF16))
        return dot(jnp.concatenate(outs, axis=1), lwo[layer])

    def mlp(layer, xn):
        return dot(gelu(dot(xn, lw1[layer])).astype(BF16), lw2[layer])

    kinds = (attention, mlp)

    def ln_near(u, ch):
        return ln_n.at[u, chunk(ch)]

    def source(kind, layer, u, s):
        values = zown[s]
        xn = norm(2 + 2 * layer + kind, values)
        ln_n[u] = xn.astype(F32)

        def send_ln(ch, carry):
            rc(ln_n.at[u, chunk(ch)], ln_n.at[u, chunk(ch)], s_lnn.at[u, ch], r_lnn.at[u, ch], inward).start()
            return carry

        lax.fori_loop(0, NCH, send_ln, 0)
        ac_n[u] = values + kinds[kind](layer, xn)

        def send_ac(ch, carry):
            rc(ac_n.at[u, chunk(ch)], ac_n.at[u, chunk(ch)], s_acn.at[u, ch], r_acn.at[u, ch], inward).start()
            return carry

        lax.fori_loop(0, NCH, send_ac, 0)

    def sink(kind, layer, u, s):
        def wait_ln(ch, carry):
            rc(ln_f.at[u, chunk(ch)], ln_f.at[u, chunk(ch)], s_lnf.at[u, ch], r_lnf.at[u, ch], inward).wait_recv()
            return carry

        lax.fori_loop(0, NCH, wait_ln, 0)
        part = kinds[kind](layer, ln_f[u].astype(BF16))

        def wait_ac(ch, carry):
            rc(ac_f.at[u, chunk(ch)], ac_f.at[u, chunk(ch)], s_acf.at[u, ch], r_acf.at[u, ch], inward).wait_recv()
            return carry

        lax.fori_loop(0, NCH, wait_ac, 0)
        zown[s] = ac_f[u] + part

    def middle(kind, layer, u):
        def near_ln(ch, carry):
            rc(ln_n.at[u, chunk(ch)], ln_n.at[u, chunk(ch)], s_lnn.at[u, ch], r_lnn.at[u, ch], outward).wait_recv()
            rc(ln_n.at[u, chunk(ch)], ln_f.at[u, chunk(ch)], s_lnn.at[u, ch], r_lnf.at[u, ch], inward).start()
            return carry

        lax.fori_loop(0, NCH, near_ln, 0)
        zown[0] = kinds[kind](layer, ln_n[u].astype(BF16))

        def both(ch, carry):
            cp = rc(ln_f.at[u, chunk(ch)], ln_f.at[u, chunk(ch)], s_lnf.at[u, ch], r_lnf.at[u, ch], outward)
            cp.wait_recv()
            cp.start()
            rc(ac_n.at[u, chunk(ch)], ac_n.at[u, chunk(ch)], s_acn.at[u, ch], r_acn.at[u, ch], outward).wait_recv()
            ac_n[u, chunk(ch)] = ac_n[u, chunk(ch)] + zown[0, chunk(ch)]
            rc(ac_n.at[u, chunk(ch)], ac_f.at[u, chunk(ch)], s_acn.at[u, ch], r_acf.at[u, ch], inward).start()
            return carry

        lax.fori_loop(0, NCH, both, 0)
        zown[1] = kinds[kind](layer, ln_f[u].astype(BF16))

        def far_ac(ch, carry):
            cp = rc(ac_f.at[u, chunk(ch)], ac_f.at[u, chunk(ch)], s_acf.at[u, ch], r_acf.at[u, ch], outward)
            cp.wait_recv()
            ac_f[u, chunk(ch)] = ac_f[u, chunk(ch)] + zown[1, chunk(ch)]
            cp.start()
            return carry

        lax.fori_loop(0, NCH, far_ac, 0)

    def line_seq(i, e):
        return y * 8 + c * 4 + i * 2 + e

    def ag_copy(b, ch, sems, dev):
        return rc(zall.at[b, chunk(ch)], zall.at[b, chunk(ch)], sems.at[b, ch], r_ag.at[b, ch], dev)

    def ag_send(b, ch, z_dev):
        if z_dev is not None:
            ag_copy(b, ch, s_agz, z_dev).start()
        ag_copy(b, ch, s_agy, y_peer).start()
        ag_copy(b, ch, s_agc, core_peer).start()

    def ag_source(i):
        b = line_seq(i, e_near)
        zall[b] = norm(6, zown[i]).astype(F32)

        def step(ch, carry):
            ag_send(b, ch, inward)
            return carry

        lax.fori_loop(0, NCH, step, 0)

    def ag_relay(i, e, z_dev):
        b = line_seq(i, e)

        def step(ch, carry):
            ag_copy(b, ch, s_agz, inward).wait_recv()
            ag_send(b, ch, z_dev)
            return carry

        lax.fori_loop(0, NCH, step, 0)

    def ag_cross(i, e):
        b = (1 - y) * 8 + c * 4 + i * 2 + e

        def step(ch, carry):
            ag_copy(b, ch, s_agy, y_peer).wait_recv()
            ag_copy(b, ch, s_agc, core_peer).start()
            return carry

        lax.fori_loop(0, NCH, step, 0)

    y_add(0)

    @pl.when(is_end)
    def _():
        z_end_send(0)

    @pl.when(is_mid)
    def _():
        z_mid(0)

    y_add(1)
    for load in loads:
        load.wait()

    @pl.when(is_end)
    def _():
        z_end_send(1)

        def start(s, carry):
            both = jnp.concatenate(split_bf16(z_end_recv(s)), axis=0)
            both = dot(both, wv[...])
            attended = (both[0:n] + both[n:2 * n]).astype(BF16)
            z = lat_ref[...].astype(F32) + dot(attended, wo[...])
            zown[s] = z + dot(gelu(dot(norm(1, z), emlp[0])).astype(BF16), emlp[1])
            source(0, 0, s, s)
            return carry

        lax.fori_loop(0, 2, start, 0)

        def layer_step(layer, carry):
            def attn_unit(s, inner):
                u = layer * 4 + s
                sink(0, layer, u, s)
                source(1, layer, u + 2, s)
                return inner

            lax.fori_loop(0, 2, attn_unit, 0)

            def mlp_unit(s, inner):
                u = layer * 4 + 2 + s
                sink(1, layer, u, s)

                @pl.when(layer == 0)
                def _():
                    source(0, 1, u + 2, s)

                @pl.when(layer == 1)
                def _():
                    ag_source(s)

                return inner

            lax.fori_loop(0, 2, mlp_unit, 0)
            return carry

        lax.fori_loop(0, 2, layer_step, 0)

    @pl.when(is_mid)
    def _():
        z_mid(1)

        def layer_step(layer, carry):
            for kind in range(2):
                def unit(s, inner):
                    middle(kind, layer, layer * 4 + 2 * kind + s)
                    return inner
                lax.fori_loop(0, 2, unit, 0)
            return carry

        lax.fori_loop(0, 2, layer_step, 0)

    def gather(i, carry):
        @pl.when(is_mid)
        def _():
            ag_relay(i, e_near, inward)
            ag_relay(i, e_far, outward)

        @pl.when(is_end)
        def _():
            ag_relay(i, e_far, None)

        ag_cross(i, e_near)
        ag_cross(i, e_far)
        return carry

    lax.fori_loop(0, 2, gather, 0)

    def last(k, carry):
        for yb in range(2):
            b = yb * 8 + (1 - c) * 4 + k

            def step(ch, inner):
                ag_copy(b, ch, s_agc, core_peer).wait_recv()
                return inner

            lax.fori_loop(0, NCH, step, 0)
        return carry

    lax.fori_loop(0, 4, last, 0)

    def convert(b, carry):
        out_ref[b] = zall[b].astype(BF16)
        return carry

    lax.fori_loop(0, 16, convert, 0)

    def done_stats(p, carry):
        g, dev = peer(p)
        rc(st_ref, st_all.at[me], s_st.at[g], r_st.at[me], dev).wait_send()
        return carry

    lax.fori_loop(1, 16, done_stats, 0)
    for i in range(2):
        core_copy(i, 1 - y).wait_send()
        core_copy(i, y).wait_send()
        for e in range(2):
            y_copy(i, e).wait_send()

    def done_z(i, carry):
        def step(ch, inner):
            rc(rz_a.at[i, chunk(ch)], rz_a.at[i, chunk(ch)], s_za.at[i, ch], r_za.at[i, ch], inward).wait_send()

            @pl.when(is_mid)
            def _():
                rc(rz_b.at[i, chunk(ch)], rz_b.at[i, chunk(ch)], s_zb.at[i, ch], r_zb.at[i, ch], outward).wait_send()

            return inner

        lax.fori_loop(0, NCH, step, 0)
        return carry

    lax.fori_loop(0, 2, done_z, 0)

    def done_units(u, carry):
        def step(ch, inner):
            rc(ln_n.at[u, chunk(ch)], ln_n.at[u, chunk(ch)], s_lnn.at[u, ch], r_lnn.at[u, ch], inward).wait_send()
            rc(ac_n.at[u, chunk(ch)], ac_n.at[u, chunk(ch)], s_acn.at[u, ch], r_acn.at[u, ch], inward).wait_send()

            @pl.when(is_mid)
            def _():
                rc(ln_f.at[u, chunk(ch)], ln_f.at[u, chunk(ch)], s_lnf.at[u, ch], r_lnf.at[u, ch], outward).wait_send()
                rc(ac_f.at[u, chunk(ch)], ac_f.at[u, chunk(ch)], s_acf.at[u, ch], r_acf.at[u, ch], outward).wait_send()

            return inner

        lax.fori_loop(0, NCH, step, 0)
        return carry

    lax.fori_loop(0, 8, done_units, 0)

    def done_ag(i, carry):
        for e in range(2):
            b = line_seq(i, e)
            other = (1 - y) * 8 + c * 4 + i * 2 + e

            def step(ch, inner):
                ag_copy(b, ch, s_agy, y_peer).wait_send()
                ag_copy(b, ch, s_agc, core_peer).wait_send()
                ag_copy(other, ch, s_agc, core_peer).wait_send()

                @pl.when(jnp.logical_or(is_mid, e == e_near))
                def _():
                    ag_copy(b, ch, s_agz, inward).wait_send()

                return inner

            lax.fori_loop(0, NCH, step, 0)
        return carry

    lax.fori_loop(0, 2, done_ag, 0)


def latent_all(num, stats, latents, norm_lat, enc_wkv, enc_wo, enc_mlp, wqkv, lwo, lw1, lw2):
    nb, n, dim = num.shape
    vm = pl.BlockSpec(memory_space=pltpu.VMEM)
    hbm = pl.BlockSpec(memory_space=pl.ANY)
    dma = pltpu.SemaphoreType.DMA
    buf = lambda *shape: pltpu.VMEM(shape + (n, dim), F32)
    return pl.pallas_call(
        latent_kernel,
        in_specs=[vm] * 4 + [hbm] * 7,
        out_specs=vm,
        out_shape=jax.ShapeDtypeStruct((nb, n, dim), BF16),
        scratch_shapes=[
            pltpu.VMEM((dim, dim), BF16), pltpu.VMEM((dim, dim), BF16), pltpu.VMEM(enc_mlp.shape, BF16),
            pltpu.VMEM(wqkv.shape, BF16), pltpu.VMEM(lwo.shape, BF16), pltpu.VMEM(lw1.shape, BF16), pltpu.VMEM(lw2.shape, BF16),
            dma((7,)),
            pltpu.VMEM((16, nb, LANES), F32), pltpu.VMEM((LANES, LANES), F32),
            buf(2, 2, 2), buf(2, 2), buf(2, 2), buf(2, 2), buf(2), buf(2),
            buf(8), buf(8), buf(8), buf(8), buf(2), buf(nb),
            dma((16,)), dma((16,)), dma((2, 2)), dma((2, 2)), dma((2, 2)), dma((2, 2)),
            dma((2, NCH)), dma((2, NCH)), dma((2, NCH)), dma((2, NCH)),
        ] + [dma((8, NCH))] * 8 + [dma((nb, NCH))] * 4,
        compiler_params=pltpu.CompilerParams(vmem_limit_bytes=VMEM_LIMIT, collective_id=0, has_side_effects=True),
        name='latent_all',
    )(num, stats, latents, norm_lat, enc_wkv, enc_wo, enc_mlp, wqkv, lwo, lw1, lw2)


def decoder_kernel(q_ref, zn_ref, nq_ref, nm_ref, wq_ref, wkv_ref, wo_ref, mlp_ref, wout_ref, y_ref, kq_s, vo_s):
    b = pl.program_id(0)
    nb, n, dim = zn_ref.shape

    @pl.when(b == 0)
    def _():
        def prepare(k, carry):
            zn = zn_ref[pl.ds(k * 4, 4)].reshape(4 * n, dim)
            high, low = split_bf16(dot_t(dot(zn, wkv_ref[0]).astype(BF16), wq_ref[...]))
            kq_s[pl.ds(k * 4, 4), 0:n, :] = high.reshape(4, n, dim)
            kq_s[pl.ds(k * 4, 4), n:2 * n, :] = low.reshape(4, n, dim)
            high, low = split_bf16(dot(dot(zn, wkv_ref[1]).astype(BF16), wo_ref[...]))
            vo_s[pl.ds(k * 4, 4), 0:n, :] = high.reshape(4, n, dim)
            vo_s[pl.ds(k * 4, 4), n:2 * n, :] = low.reshape(4, n, dim)
            return carry

        lax.fori_loop(0, nb // 4, prepare, 0)

    xq = layer_norm(q_ref[0].astype(F32), nq_ref[0:1, :], nq_ref[1:2, :])
    both = dot_t(xq, kq_s[b])
    scores = (both + pltpu.roll(both, n, 1)) * (1.0 / math.sqrt(dim))
    weights = jnp.exp(scores - jnp.max(scores, axis=1, keepdims=True))
    probs = (weights / (0.5 * jnp.sum(weights, axis=1, keepdims=True))).astype(BF16)
    u = dot(probs, vo_s[b])
    hidden = gelu(dot(layer_norm(u, nm_ref[0:1, :], nm_ref[1:2, :]), mlp_ref[0])).astype(BF16)
    u = u + dot(hidden, mlp_ref[1])
    y_ref[0] = dot(u.astype(BF16), wout_ref[...])


def decoder(q_loc, zn, norm_query, norm_mlp, dec_wq, dec_wkv, dec_wo, dec_mlp, dec_out):
    nb, rows, dim = q_loc.shape
    n = zn.shape[1]
    whole = lambda shape: pl.BlockSpec(shape, lambda b: (0,) * len(shape), pipeline_mode=pl.Buffered(1))
    return pl.pallas_call(
        decoder_kernel,
        grid=(nb,),
        in_specs=[pl.BlockSpec((1, rows, dim), lambda b: (b, 0, 0)), whole(zn.shape), whole((2, dim)), whole((2, dim)),
                  whole((dim, dim)), whole((2, dim, dim)), whole((dim, dim)), whole((2, dim, dim)), whole((dim, dim))],
        out_specs=pl.BlockSpec((1, rows, dim), lambda b: (b, 0, 0)),
        out_shape=jax.ShapeDtypeStruct((nb, rows, dim), F32),
        scratch_shapes=[pltpu.VMEM((nb, 2 * n, dim), BF16), pltpu.VMEM((nb, 2 * n, dim), BF16)],
        compiler_params=pltpu.CompilerParams(vmem_limit_bytes=VMEM_LIMIT),
        name='dec_local',
    )(q_loc, zn, norm_query, norm_mlp, dec_wq, dec_wkv, dec_wo, dec_mlp, dec_out)


def solution(mesh):
    seq_spec = P('dp', ('tp', 'sp'), None)
    replicated = P()
    in_specs = (seq_spec, seq_spec, replicated, replicated, replicated, replicated, replicated, replicated, replicated, replicated,
                P(None, None, None, 'tp', None), P(None, 'tp', None, None), P(None, None, 'tp'), P(None, 'tp', None),
                replicated, replicated, replicated, replicated, replicated)

    def device_step(x_loc, q_loc, latents, norm_in, norm_query, norm_lat, enc_wq, enc_wkv, enc_wo, enc_mlp,
                    lat_wqkv, lat_wo, lat_w1, lat_w2, dec_wq, dec_wkv, dec_wo, dec_mlp, dec_out):
        layers, dim = lat_wqkv.shape[0], latents.shape[1]
        wqkv = lat_wqkv.reshape(layers, dim, -1)
        lwo = lat_wo.reshape(layers, -1, dim)
        num, stats = encoder_local(x_loc, norm_in, latents, norm_lat[0], enc_wq, enc_wkv)
        zn = latent_all(num, stats, latents, norm_lat, enc_wkv, enc_wo, enc_mlp, wqkv, lwo, lat_w1, lat_w2)
        return decoder(q_loc, zn, norm_query, norm_lat[7], dec_wq, dec_wkv, dec_wo, dec_mlp, dec_out)

    return jax.shard_map(device_step, mesh=mesh, in_specs=in_specs, out_specs=seq_spec, check_vma=False)
```

time: 1000 us -> 282 us (0.28)
  waiting for transfers between devices: 672 us -> 0 us
  Pallas kernels: 0 us -> 271 us
  matrix products: 171 us -> 0 us
  blocking collectives: 67.3 us -> 0 us
  other arithmetic: 49.6 us -> 0 us
  between operations: 14.2 us -> 0.01 us
    psum x5 -> x0, waiting for transfers between devices: 672 us -> none  [the longest x2 305 us: device_step(): latent = latent + lax.psum(att_sum, 'tp')]
    pallas_call x0 -> x3, Pallas kernels: none -> 271 us  [the longest x1 180 us: latent_all(): pl.pallas_call(latent_kernel, in_specs=[vm] * 4 + [hbm] * 7, out_specs=vm...]
    dot_general x19 -> x0, matrix products: 168 us -> none  [the longest x4 54.5 us: mlp_part(): jnp.einsum('bnf,fe->bne', hidden.astype(jnp.bfloat16), w_down, preferred_...]
    reduce_sum x18 -> x0, other arithmetic: 49.2 us -> none  [the longest x7 26.3 us: layer_norm(): row_mean = jnp.mean(val_f32, axis=-1, keepdims=True)]
    pmax x1 -> x0, blocking collectives: 35.7 us -> none  [device_step(): row_max = lax.pmax(jnp.max(scores, axis=2, keepdims=True), GROUP_AXES)]
    psum x1 -> x0, blocking collectives: 31.6 us -> none  [device_step(): lax.psum((local_num, jnp.sum(weights, axis=2, keepdims=True)), GROUP_AXES)]
    unnamed x50 -> x0, local copies, waits for them, and re-layouts: 11.8 us -> none
  transfers between devices with their start and end apart: 5 -> 0, of which waited for: 5 -> 0; matrix products, arithmetic and copies ran while one was open for 2% -> 0% of each run, Pallas kernels for 0% -> 0%
where the time goes in v1:
time: 282 us; the launch traced here: 281 us
  Pallas kernels  271 us (96%)
  local copies, waits for them, and re-layouts  9.37 us (3%)
    pallas_call x1, Pallas kernels, latent_all(): pl.pallas_call(latent_kernel, in_specs=[vm] * 4 + [hbm] * 7, out_specs=vm...  180 us
    pallas_call x1, Pallas kernels, decoder(): pl.pallas_call(decoder_kernel, grid=(nb,), in_specs=[pl.BlockSpec((1, row...  69.9 us
    pallas_call x1, Pallas kernels, encoder_local(): pl.pallas_call(encoder_kernel, grid=(nb,), in_specs=[pl.BlockSpec((1, row...  21.4 us
    reshape x1, local copies, waits for them, and re-layouts, device_step(): wqkv = lat_wqkv.reshape(layers, dim, -1)  8.04 us

profile of v1, /device:TPU:0, one launch (start us, length us, event | category | flops | bytes accessed | tf_op | source)
XLA Modules:
  0.0 280.7 jit_solution(11205144615423718913)
XLA Ops:
  0.0 1.3 slice_bitcast_fusion
  1.3 8.0 %reshape.6.qkv_h = bf16[2,1024,768]{2,1,0:T(8,128)(2,1)} reshape(bf16[2,1024,3,2,128]{4,3,2,1,0:T(2,128)(2,1)} %param.29) | data formatting | bytes 6291456 | tf_op jit(solution)/shard_map/reshape | solution.py:614
  9.4 21.4 %enc_local.1 = (f32[16,64,1024]{2,1,0:T(8,128)}, f32[16,128]{1,0:T(8,128)}) custom-call(bf16[16,256,1024]{2,1,0:T(8,128)(2,1)} %x_ref.1, f32[2,1024]{1,0:T(2,128)} %nin_ref.1, bf16[64,1024]{1,0:T(8,128)(2,1)} %lat_ref.3, f32[2,1024]{1,0:T(2,128)} %get-tuple-element.10.nq_ref, bf16[1024,1024]{1,0:T(8,128)(2,1)} %wq_ref.2, bf16[2,1024,1024]{2,1,0:T(8,128)(2,1)} %wkv_h.1), custom_call_target="tpu_custom_call" | custom-call | tf_op jit(solution)/shard_map/enc_local/pallas_call | solution.py:77
  30.8 180.0 %latent_all.1.zn_ref = bf16[16,64,1024]{2,1,0:T(8,128)(2,1)} custom-call(f32[16,64,1024]{2,1,0:T(8,128)} %get-tuple-element.7.num_ref, f32[16,128]{1,0:T(8,128)} %get-tuple-element.8.st_ref, bf16[64,1024]{1,0:T(8,128)(2,1)} %lat_ref.3, f32[8,2,1024]{2,1,0:T(2,128)} %nlat_ref.1, bf16[2,1024,1024]{2,1,0:T(8,128)(2,1)} %wkv_h.1, bf16[1024,1024]{1,0:T(8,128)(2,1)} %wo_h.1, ...), custom_call_target="tpu_custom_call" | custom-call | tf_op jit(solution)/shard_map/latent_all/pallas_call | solution.py:538
  210.8 69.9 %dec_local.1 = f32[16,256,1024]{2,1,0:T(8,128)} custom-call(bf16[16,256,1024]{2,1,0:T(8,128)(2,1)} %q_ref.1, bf16[16,64,1024]{2,1,0:T(8,128)(2,1)} %latent_all.1.zn_ref, f32[2,1024]{1,0:T(2,128)} %nq_ref.1, f32[2,1024]{1,0:T(2,128)} %get-tuple-element.9.nm_ref, bf16[1024,1024]{1,0:T(8,128)(2,1)} %wq_ref.3, bf16[2,1024,1024]{2,1,0:T(8,128)(2,1)} %wkv_ref.1, ...), custom_call_target="tpu_custom_call" | custom-call | tf_op jit(solution)/shard_map/dec_local/pallas_call | solution.py:591

commit v2 on v1

--- a/solution.py
+++ b/solution.py
@@ -13,6 +13,8 @@
 VMEM_LIMIT = 60 * 1024 * 1024
 LANES = 128
 NLINE = 4
+RBLK = 128
+ENC_STEP = 4
 NCH = 4
 GELU_C = math.sqrt(2.0 / math.pi)
 
@@ -54,16 +56,18 @@
         qk_s[n:2 * n, :] = low
         stats_s[...] = jnp.zeros_like(stats_s)
 
-    xn = layer_norm(x_ref[0].astype(F32), nin_ref[0:1, :], nin_ref[1:2, :])
-    both = dot_t(qk_s[...], xn)
-    scores = (both[:n] + both[n:]) * (1.0 / math.sqrt(dim))
-    row_max = jnp.max(scores, axis=1, keepdims=True)
-    weights = jnp.exp(scores - row_max)
-    row_sum = jnp.sum(weights, axis=1, keepdims=True)
-    num_ref[0] = dot(weights.astype(BF16), xn)
-    here = lax.broadcasted_iota(jnp.int32, (n, LANES), 1) == b
-    stats_s[0:n, :] = jnp.where(here, row_max, stats_s[0:n, :])
-    stats_s[n:2 * n, :] = jnp.where(here, row_sum, stats_s[n:2 * n, :])
+    each = range(x_ref.shape[0])
+    xns = [layer_norm(x_ref[j].astype(F32), nin_ref[0:1, :], nin_ref[1:2, :]) for j in each]
+    both = [dot_t(qk_s[...], xn) for xn in xns]
+    scores = [(v[:n] + v[n:]) * (1.0 / math.sqrt(dim)) for v in both]
+    maxima = [jnp.max(v, axis=1, keepdims=True) for v in scores]
+    weights = [jnp.exp(v - m) for v, m in zip(scores, maxima)]
+    sums = [jnp.sum(v, axis=1, keepdims=True) for v in weights]
+    for j in each:
+        num_ref[j] = dot(weights[j].astype(BF16), xns[j])
+        here = lax.broadcasted_iota(jnp.int32, (n, LANES), 1) == b * x_ref.shape[0] + j
+        stats_s[0:n, :] = jnp.where(here, maxima[j], stats_s[0:n, :])
+        stats_s[n:2 * n, :] = jnp.where(here, sums[j], stats_s[n:2 * n, :])
 
     @pl.when(b == pl.num_programs(0) - 1)
     def _():
@@ -76,10 +80,10 @@
     whole = lambda shape: pl.BlockSpec(shape, lambda b: (0,) * len(shape))
     return pl.pallas_call(
         encoder_kernel,
-        grid=(nb,),
-        in_specs=[pl.BlockSpec((1, rows, dim), lambda b: (b, 0, 0)), whole((2, dim)), whole((n, dim)), whole((2, dim)),
+        grid=(nb // ENC_STEP,),
+        in_specs=[pl.BlockSpec((ENC_STEP, rows, dim), lambda b: (b, 0, 0)), whole((2, dim)), whole((n, dim)), whole((2, dim)),
                   whole((dim, dim)), pl.BlockSpec((1, dim, dim), lambda b: (0, 0, 0))],
-        out_specs=[pl.BlockSpec((1, n, dim), lambda b: (b, 0, 0)), whole((nb, LANES))],
+        out_specs=[pl.BlockSpec((ENC_STEP, n, dim), lambda b: (b, 0, 0)), whole((nb, LANES))],
         out_shape=[jax.ShapeDtypeStruct((nb, n, dim), F32), jax.ShapeDtypeStruct((nb, LANES), F32)],
         scratch_shapes=[pltpu.VMEM((2 * n, dim), BF16), pltpu.VMEM((LANES, LANES), F32)],
         compiler_params=pltpu.CompilerParams(vmem_limit_bytes=VMEM_LIMIT),
@@ -233,11 +237,11 @@
         return layer_norm(values, nlat_ref[index, 0:1, :], nlat_ref[index, 1:2, :])
 
     def attention(layer, xn):
-        hd = wqkv.shape[2] // 6
-        qkv = dot(xn, wqkv[layer]).astype(BF16)
+        hd = wqkv.shape[4]
+        qkv = [dot(xn, jnp.concatenate([wqkv[layer, j, 0], wqkv[layer, j, 1]], axis=1)).astype(BF16) for j in range(3)]
         outs = []
         for h in range(2):
-            q, k, v = (qkv[:, (2 * j + h) * hd:(2 * j + h + 1) * hd] for j in range(3))
+            q, k, v = (part[:, h * hd:(h + 1) * hd] for part in qkv)
             scores = dot_t(q, k) * (1.0 / math.sqrt(hd))
             weights = jnp.exp(scores - jnp.max(scores, axis=1, keepdims=True))
             probs = (weights / jnp.sum(weights, axis=1, keepdims=True)).astype(BF16)
@@ -555,7 +559,7 @@
     )(num, stats, latents, norm_lat, enc_wkv, enc_wo, enc_mlp, wqkv, lwo, lw1, lw2)
 
 
-def decoder_kernel(q_ref, zn_ref, nq_ref, nm_ref, wq_ref, wkv_ref, wo_ref, mlp_ref, wout_ref, y_ref, kq_s, vo_s):
+def decoder_kernel(q_ref, zn_ref, nq_ref, nm_ref, wq_ref, wkv_ref, wo_ref, mlp_ref, wout_ref, y_ref, kq_s, vo_s, xu_s, u_s, p_s):
     b = pl.program_id(0)
     nb, n, dim = zn_ref.shape
 
@@ -572,16 +576,38 @@
             return carry
 
         lax.fori_loop(0, nb // 4, prepare, 0)
-
-    xq = layer_norm(q_ref[0].astype(F32), nq_ref[0:1, :], nq_ref[1:2, :])
-    both = dot_t(xq, kq_s[b])
-    scores = (both + pltpu.roll(both, n, 1)) * (1.0 / math.sqrt(dim))
-    weights = jnp.exp(scores - jnp.max(scores, axis=1, keepdims=True))
-    probs = (weights / (0.5 * jnp.sum(weights, axis=1, keepdims=True))).astype(BF16)
-    u = dot(probs, vo_s[b])
-    hidden = gelu(dot(layer_norm(u, nm_ref[0:1, :], nm_ref[1:2, :]), mlp_ref[0])).astype(BF16)
-    u = u + dot(hidden, mlp_ref[1])
-    y_ref[0] = dot(u.astype(BF16), wout_ref[...])
+        xu_s[...] = jnp.zeros_like(xu_s)
+        u_s[...] = jnp.zeros_like(u_s)
+
+    ahead = lax.rem(b, 2)
+    now = 1 - ahead
+    seq = jnp.minimum(b, nb - 1)
+    rows = q_ref.shape[1]
+    nblk = rows // RBLK
+    cblk = dim // nblk
+    xu = xu_s[now]
+    hidden = []
+    for k in range(nblk):
+        part = pl.ds(k * RBLK, RBLK)
+        cols = slice(k * cblk, (k + 1) * cblk)
+        hidden.append(gelu(dot(xu, mlp_ref[0, :, cols])).astype(BF16))
+        xq = layer_norm(q_ref[0, part].astype(F32), nq_ref[0:1, :], nq_ref[1:2, :])
+        both = dot_t(xq, kq_s[seq])
+        scores = (both + pltpu.roll(both, n, 1)) * (1.0 / math.sqrt(dim))
+        weights = jnp.exp(scores - jnp.max(scores, axis=1, keepdims=True))
+        probs = (weights / (0.5 * jnp.sum(weights, axis=1, keepdims=True))).astype(BF16)
+        p_s[part] = probs
+    hidden = jnp.concatenate(hidden, axis=1)
+    out = []
+    for k in range(nblk):
+        part = pl.ds(k * RBLK, RBLK)
+        cols = slice(k * cblk, (k + 1) * cblk)
+        out.append((u_s[now, :, cols] + dot(hidden, mlp_ref[1, :, cols])).astype(BF16))
+        u = dot(p_s[part], vo_s[seq])
+        u_s[ahead, part] = u
+        xu_s[ahead, part] = layer_norm(u, nm_ref[0:1, :], nm_ref[1:2, :])
+    out = jnp.concatenate(out, axis=1)
+    y_ref[0] = dot(out, wout_ref[...])
 
 
 def decoder(q_loc, zn, norm_query, norm_mlp, dec_wq, dec_wkv, dec_wo, dec_mlp, dec_out):
@@ -590,12 +616,13 @@
     whole = lambda shape: pl.BlockSpec(shape, lambda b: (0,) * len(shape), pipeline_mode=pl.Buffered(1))
     return pl.pallas_call(
         decoder_kernel,
-        grid=(nb,),
-        in_specs=[pl.BlockSpec((1, rows, dim), lambda b: (b, 0, 0)), whole(zn.shape), whole((2, dim)), whole((2, dim)),
+        grid=(nb + 1,),
+        in_specs=[pl.BlockSpec((1, rows, dim), lambda b: (jnp.minimum(b, nb - 1), 0, 0)), whole(zn.shape), whole((2, dim)), whole((2, dim)),
                   whole((dim, dim)), whole((2, dim, dim)), whole((dim, dim)), whole((2, dim, dim)), whole((dim, dim))],
-        out_specs=pl.BlockSpec((1, rows, dim), lambda b: (b, 0, 0)),
+        out_specs=pl.BlockSpec((1, rows, dim), lambda b: (jnp.maximum(b - 1, 0), 0, 0)),
         out_shape=jax.ShapeDtypeStruct((nb, rows, dim), F32),
-        scratch_shapes=[pltpu.VMEM((nb, 2 * n, dim), BF16), pltpu.VMEM((nb, 2 * n, dim), BF16)],
+        scratch_shapes=[pltpu.VMEM((nb, 2 * n, dim), BF16), pltpu.VMEM((nb, 2 * n, dim), BF16),
+                        pltpu.VMEM((2, rows, dim), BF16), pltpu.VMEM((2, rows, dim), F32), pltpu.VMEM((rows, LANES), BF16)],
         compiler_params=pltpu.CompilerParams(vmem_limit_bytes=VMEM_LIMIT),
         name='dec_local',
     )(q_loc, zn, norm_query, norm_mlp, dec_wq, dec_wkv, dec_wo, dec_mlp, dec_out)
@@ -611,7 +638,7 @@
     def device_step(x_loc, q_loc, latents, norm_in, norm_query, norm_lat, enc_wq, enc_wkv, enc_wo, enc_mlp,
                     lat_wqkv, lat_wo, lat_w1, lat_w2, dec_wq, dec_wkv, dec_wo, dec_mlp, dec_out):
         layers, dim = lat_wqkv.shape[0], latents.shape[1]
-        wqkv = lat_wqkv.reshape(layers, dim, -1)
+        wqkv = lat_wqkv.transpose(0, 2, 3, 1, 4)
         lwo = lat_wo.reshape(layers, -1, dim)
         num, stats = encoder_local(x_loc, norm_in, latents, norm_lat[0], enc_wq, enc_wkv)
         zn = latent_all(num, stats, latents, norm_lat, enc_wkv, enc_wo, enc_mlp, wqkv, lwo, lat_w1, lat_w2)

time: 282 us -> 257 us (0.911)
  Pallas kernels: 271 us -> 251 us
  local copies, waits for them, and re-layouts: 9.37 us -> 5.38 us
    pallas_call x2, Pallas kernels: 91.3 us -> 70.7 us  [the longest x1 57.3 us: decoder(): pl.pallas_call(decoder_kernel, grid=(nb + 1,), in_specs=[pl.BlockSpec((1,...]
    reshape x1 -> x0, local copies, waits for them, and re-layouts: 8.04 us -> none  [device_step(): wqkv = lat_wqkv.reshape(layers, dim, -1)]
    unnamed x0 -> x1, local copies, waits for them, and re-layouts: none -> 4.05 us
where the time goes in v2:
time: 257 us; the launch traced here: 256 us
  Pallas kernels  251 us (98%)
  local copies, waits for them, and re-layouts  5.38 us (2%)
    pallas_call x1, Pallas kernels, latent_all(): pl.pallas_call(latent_kernel, in_specs=[vm] * 4 + [hbm] * 7, out_specs=vm...  180 us
    pallas_call x1, Pallas kernels, decoder(): pl.pallas_call(decoder_kernel, grid=(nb + 1,), in_specs=[pl.BlockSpec((1,...  57.3 us
    pallas_call x1, Pallas kernels, encoder_local(): pl.pallas_call(encoder_kernel, grid=(nb // ENC_STEP,), in_specs=[pl.Block...  13.4 us

profile of v2, /device:TPU:0, one launch (start us, length us, event | category | flops | bytes accessed | tf_op | source)
XLA Modules:
  0.0 256.1 jit_solution(5543916567508303199)
XLA Ops:
  0.0 1.3 slice_bitcast_fusion
  1.3 4.1 %copy.22 = bf16[2,1024,3,2,128]{4,1,3,2,0:T(8,128)(2,1)} copy(bf16[2,1024,3,2,128]{4,3,2,1,0:T(2,128)(2,1)} %param.29) | data formatting | bytes 6291456 | tf_op args[10]
  5.4 13.4 %enc_local.1 = (f32[16,64,1024]{2,1,0:T(8,128)}, f32[16,128]{1,0:T(8,128)}) custom-call(bf16[16,256,1024]{2,1,0:T(8,128)(2,1)} %x_ref.1, f32[2,1024]{1,0:T(2,128)} %nin_ref.1, bf16[64,1024]{1,0:T(8,128)(2,1)} %lat_ref.3, f32[2,1024]{1,0:T(2,128)} %get-tuple-element.10.nq_ref, bf16[1024,1024]{1,0:T(8,128)(2,1)} %wq_ref.2, bf16[2,1024,1024]{2,1,0:T(8,128)(2,1)} %wkv_h.1), custom_call_target="tpu_custom_call" | custom-call | tf_op jit(solution)/shard_map/enc_local/pallas_call | solution.py:81
  18.8 180.0 %latent_all.1.zn_ref = bf16[16,64,1024]{2,1,0:T(8,128)(2,1)} custom-call(f32[16,64,1024]{2,1,0:T(8,128)} %get-tuple-element.7.num_ref, f32[16,128]{1,0:T(8,128)} %get-tuple-element.8.st_ref, bf16[64,1024]{1,0:T(8,128)(2,1)} %lat_ref.3, f32[8,2,1024]{2,1,0:T(2,128)} %nlat_ref.1, bf16[2,1024,1024]{2,1,0:T(8,128)(2,1)} %wkv_h.1, bf16[1024,1024]{1,0:T(8,128)(2,1)} %wo_h.1, ...), custom_call_target="tpu_custom_call" | custom-call | tf_op jit(solution)/shard_map/latent_all/pallas_call | solution.py:542
  198.8 57.3 %dec_local.1 = f32[16,256,1024]{2,1,0:T(8,128)} custom-call(bf16[16,256,1024]{2,1,0:T(8,128)(2,1)} %q_ref.1, bf16[16,64,1024]{2,1,0:T(8,128)(2,1)} %latent_all.1.zn_ref, f32[2,1024]{1,0:T(2,128)} %nq_ref.1, f32[2,1024]{1,0:T(2,128)} %get-tuple-element.9.nm_ref, bf16[1024,1024]{1,0:T(8,128)(2,1)} %wq_ref.3, bf16[2,1024,1024]{2,1,0:T(8,128)(2,1)} %wkv_ref.1, ...), custom_call_target="tpu_custom_call" | custom-call | tf_op jit(solution)/shard_map/dec_local/pallas_call | solution.py:617

commit v3 on v2

--- a/solution.py
+++ b/solution.py
@@ -10,10 +10,11 @@
 LN_EPS = 1e-5
 F32, BF16 = jnp.float32, jnp.bfloat16
 MESH = pl.DeviceIdType.MESH
-VMEM_LIMIT = 60 * 1024 * 1024
+VMEM_LIMIT = 63 * 1024 * 1024
 LANES = 128
 NLINE = 4
 RBLK = 128
+OUT_STEP = 2
 ENC_STEP = 4
 NCH = 4
 GELU_C = math.sqrt(2.0 / math.pi)
@@ -91,8 +92,10 @@
     )(x_loc, norm_in, latents, norm_q, enc_wq, enc_wkv)
 
 
-def latent_kernel(num_ref, st_ref, lat_ref, nlat_ref, wkv_h, wo_h, emlp_h, qkv_h, lwo_h, lw1_h, lw2_h, out_ref,
-                  wv, wo, emlp, wqkv, lwo, lw1, lw2, wsem,
+def latent_kernel(num_ref, st_ref, lat_ref, nlat_ref, nq_ref, wkv_h, wo_h, emlp_h, qkv_h, lwo_h, lw1_h, lw2_h,
+                  q_h, dwq_h, dwkv_h, dwo_h, dmlp_h, out_h,
+                  wv, wo, emlp, wqkv, lwo, lw1, lw2, wsem, wkq, wvo,
+                  kq_s, vo_s, xu_s, u_s, p_s, qbuf, ubuf, qsem, usem,
                   st_all, gs, d2d, ysend, yrecv, zsum, rz_a, rz_b, ln_n, ln_f, ac_n, ac_f, zown, zall,
                   s_st, r_st, s_d2, r_d2, s_y, r_y, s_za, s_zb, r_za, r_zb,
                   s_lnn, s_lnf, s_acn, s_acf, r_lnn, r_lnf, r_acn, r_acf, r_ag, s_agz, s_agc, s_agy):
@@ -122,10 +125,14 @@
         g = lax.rem(me + p, 16)
         return g, (x, lax.div(g, 4), lax.rem(g, 4))
 
-    loads = [pltpu.make_async_copy(src, dst, wsem.at[i]) for i, (src, dst) in enumerate(
-        ((wkv_h.at[1], wv), (wo_h, wo), (emlp_h, emlp), (qkv_h, wqkv), (lwo_h, lwo), (lw1_h, lw1), (lw2_h, lw2)))]
-    for load in loads:
-        load.start()
+    def fetch(first, pairs):
+        copies = [pltpu.make_async_copy(src, dst, wsem.at[first + k]) for k, (src, dst) in enumerate(pairs)]
+        for copy in copies:
+            copy.start()
+        return copies
+
+    dec_loads = fetch(0, ((dwkv_h, emlp), (dwq_h, wv), (dwo_h, wo)))
+    lat_loads = fetch(3, ((qkv_h, wqkv), (lwo_h, lwo), (lw1_h, lw1), (lw2_h, lw2)))
 
     barrier = pltpu.get_barrier_semaphore()
 
@@ -309,6 +316,10 @@
 
         lax.fori_loop(0, NCH, both, 0)
         zown[1] = kinds[kind](layer, ln_f[u].astype(BF16))
+        if kind == 1:
+            @pl.when(u == 7)
+            def _():
+                ag_relay(0, e_near, inward)
 
         def far_ac(ch, carry):
             cp = rc(ac_f.at[u, chunk(ch)], ac_f.at[u, chunk(ch)], s_acf.at[u, ch], r_acf.at[u, ch], outward)
@@ -361,6 +372,20 @@
 
         lax.fori_loop(0, NCH, step, 0)
 
+    for load in dec_loads:
+        load.wait()
+
+    def products(k, carry):
+        part = pl.ds(pl.multiple_of(k * 256, 256), 256)
+        wkq[part] = dot_t(emlp[0, part], wv[...]).astype(BF16)
+        wvo[part] = dot(emlp[1, part], wo[...]).astype(BF16)
+        return carry
+
+    lax.fori_loop(0, dim // 256, products, 0)
+    enc_loads = fetch(7, ((wkv_h.at[1], wv), (wo_h, wo), (emlp_h, emlp)))
+    def tail_loads():
+        return [pltpu.make_async_copy(dmlp_h, emlp, wsem.at[10])]
+
     y_add(0)
 
     @pl.when(is_end)
@@ -372,7 +397,7 @@
         z_mid(0)
 
     y_add(1)
-    for load in loads:
+    for load in lat_loads + enc_loads:
         load.wait()
 
     @pl.when(is_end)
@@ -389,6 +414,8 @@
             return carry
 
         lax.fori_loop(0, 2, start, 0)
+        for load in tail_loads():
+            load.start()
 
         def layer_step(layer, carry):
             def attn_unit(s, inner):
@@ -421,6 +448,8 @@
     @pl.when(is_mid)
     def _():
         z_mid(1)
+        for load in tail_loads():
+            load.start()
 
         def layer_step(layer, carry):
             for kind in range(2):
@@ -432,40 +461,111 @@
 
         lax.fori_loop(0, 2, layer_step, 0)
 
-    def gather(i, carry):
-        @pl.when(is_mid)
+    def order(k):
+        i = lax.div(k, 8)
+        r = lax.rem(k, 8)
+        pair = lax.div(r, 2)
+        odd = lax.rem(pair, 2)
+        yb = y + odd - 2 * y * odd
+        core = lax.rem(r, 2)
+        cb = c + core - 2 * c * core
+        far = lax.div(pair, 2)
+        e = e_near + far - 2 * e_near * far
+        return yb * 8 + cb * 4 + i * 2 + e
+
+    def q_copy(k):
+        return pltpu.make_async_copy(q_h.at[order(k)], qbuf.at[lax.rem(k, 2)], qsem.at[lax.rem(k, 2)])
+
+    def u_copy(k):
+        return pltpu.make_async_copy(ubuf.at[lax.rem(k, 2)], out_h.at[order(k)], usem.at[lax.rem(k, 2)])
+
+    q_copy(0).start()
+    for load in tail_loads():
+        load.wait()
+    xu_s[...] = jnp.zeros_like(xu_s)
+    u_s[...] = jnp.zeros_like(u_s)
+    nrow = qbuf.shape[1]
+    nblk = nrow // RBLK
+    cblk = dim // nblk
+
+    def decode(k, carry):
+        @pl.when(jnp.logical_and(lax.rem(k, 2) == 0, k < 16))
         def _():
-            ag_relay(i, e_near, inward)
-            ag_relay(i, e_far, outward)
-
-        @pl.when(is_end)
+            other = order(k + 1)
+
+            def step(ch, inner):
+                ag_copy(other, ch, s_agc, core_peer).wait_recv()
+                return inner
+
+            lax.fori_loop(0, NCH, step, 0)
+            zn = jnp.concatenate([zall[order(k)], zall[other]], axis=0).astype(BF16)
+            for weights, target in ((wkq, kq_s), (wvo, vo_s)):
+                high, low = split_bf16(dot(zn, weights[...]))
+                for j in range(2):
+                    target[j, 0:n, :] = high[j * n:(j + 1) * n]
+                    target[j, n:2 * n, :] = low[j * n:(j + 1) * n]
+
+        @pl.when(k < 16)
         def _():
-            ag_relay(i, e_far, None)
-
-        ag_cross(i, e_near)
-        ag_cross(i, e_far)
-        return carry
-
-    lax.fori_loop(0, 2, gather, 0)
-
-    def last(k, carry):
-        for yb in range(2):
-            b = yb * 8 + (1 - c) * 4 + k
-
-            def step(ch, inner):
-                ag_copy(b, ch, s_agc, core_peer).wait_recv()
-                return inner
-
-            lax.fori_loop(0, NCH, step, 0)
-        return carry
-
-    lax.fori_loop(0, 4, last, 0)
-
-    def convert(b, carry):
-        out_ref[b] = zall[b].astype(BF16)
-        return carry
-
-    lax.fori_loop(0, 16, convert, 0)
+            q_copy(k).wait()
+
+        @pl.when(k < 15)
+        def _():
+            q_copy(k + 1).start()
+
+        @pl.when(k >= 3)
+        def _():
+            u_copy(k - 3).wait()
+
+        ahead = lax.rem(k, 2)
+        now = 1 - ahead
+        xu = xu_s[now]
+        hidden = []
+        for blk in range(nblk):
+            part = pl.ds(blk * RBLK, RBLK)
+            cols = slice(blk * cblk, (blk + 1) * cblk)
+            hidden.append(gelu(dot(xu, emlp[0, :, cols])).astype(BF16))
+            xq = layer_norm(qbuf[ahead, part].astype(F32), nq_ref[0:1, :], nq_ref[1:2, :])
+            both = dot_t(xq, kq_s[ahead])
+            scores = (both + pltpu.roll(both, n, 1)) * (1.0 / math.sqrt(dim))
+            weights = jnp.exp(scores - jnp.max(scores, axis=1, keepdims=True))
+            p_s[part] = (weights / (0.5 * jnp.sum(weights, axis=1, keepdims=True))).astype(BF16)
+        hidden = jnp.concatenate(hidden, axis=1)
+        for blk in range(nblk):
+            part = pl.ds(blk * RBLK, RBLK)
+            cols = slice(blk * cblk, (blk + 1) * cblk)
+            ubuf[now, :, cols] = (u_s[now, :, cols] + dot(hidden, emlp[1, :, cols])).astype(BF16)
+            u = dot(p_s[part], vo_s[ahead])
+            u_s[ahead, part] = u
+            xu_s[ahead, part] = norm(7, u)
+
+        @pl.when(k >= 1)
+        def _():
+            u_copy(k - 1).start()
+
+        def far_relay(i):
+            @pl.when(is_mid)
+            def _():
+                ag_relay(i, e_far, outward)
+
+            @pl.when(is_end)
+            def _():
+                ag_relay(i, e_far, None)
+
+        def near_relay(i):
+            @pl.when(is_mid)
+            def _():
+                ag_relay(i, e_near, inward)
+
+        for when, what in ((0, lambda: far_relay(0)), (1, lambda: ag_cross(0, e_near)), (3, lambda: ag_cross(0, e_far)),
+                           (4, lambda: near_relay(1)), (6, lambda: far_relay(1)), (7, lambda: ag_cross(1, e_near)),
+                           (9, lambda: ag_cross(1, e_far))):
+            pl.when(k == when)(what)
+        return carry
+
+    lax.fori_loop(0, 17, decode, 0)
+    u_copy(14).wait()
+    u_copy(15).wait()
 
     def done_stats(p, carry):
         g, dev = peer(p)
@@ -533,21 +633,26 @@
     lax.fori_loop(0, 2, done_ag, 0)
 
 
-def latent_all(num, stats, latents, norm_lat, enc_wkv, enc_wo, enc_mlp, wqkv, lwo, lw1, lw2):
+def latent_all(num, stats, q_loc, latents, norm_lat, norm_query, enc_wkv, enc_wo, enc_mlp, wqkv, lwo, lw1, lw2,
+               dec_wq, dec_wkv, dec_wo, dec_mlp):
     nb, n, dim = num.shape
+    rows = q_loc.shape[1]
     vm = pl.BlockSpec(memory_space=pltpu.VMEM)
     hbm = pl.BlockSpec(memory_space=pl.ANY)
     dma = pltpu.SemaphoreType.DMA
     buf = lambda *shape: pltpu.VMEM(shape + (n, dim), F32)
+    half = lambda *shape: pltpu.VMEM(shape + (dim,), BF16)
     return pl.pallas_call(
         latent_kernel,
-        in_specs=[vm] * 4 + [hbm] * 7,
-        out_specs=vm,
-        out_shape=jax.ShapeDtypeStruct((nb, n, dim), BF16),
+        in_specs=[vm] * 5 + [hbm] * 12,
+        out_specs=hbm,
+        out_shape=jax.ShapeDtypeStruct((nb, rows, dim), BF16),
         scratch_shapes=[
-            pltpu.VMEM((dim, dim), BF16), pltpu.VMEM((dim, dim), BF16), pltpu.VMEM(enc_mlp.shape, BF16),
+            half(dim), half(dim), pltpu.VMEM(enc_mlp.shape, BF16),
             pltpu.VMEM(wqkv.shape, BF16), pltpu.VMEM(lwo.shape, BF16), pltpu.VMEM(lw1.shape, BF16), pltpu.VMEM(lw2.shape, BF16),
-            dma((7,)),
+            dma((11,)), half(dim), half(dim),
+            half(2, 2 * n), half(2, 2 * n), half(2, rows), pltpu.VMEM((2, rows, dim), F32), pltpu.VMEM((rows, LANES), BF16),
+            half(2, rows), half(2, rows), dma((2,)), dma((2,)),
             pltpu.VMEM((16, nb, LANES), F32), pltpu.VMEM((LANES, LANES), F32),
             buf(2, 2, 2), buf(2, 2), buf(2, 2), buf(2, 2), buf(2), buf(2),
             buf(8), buf(8), buf(8), buf(8), buf(2), buf(nb),
@@ -556,76 +661,26 @@
         ] + [dma((8, NCH))] * 8 + [dma((nb, NCH))] * 4,
         compiler_params=pltpu.CompilerParams(vmem_limit_bytes=VMEM_LIMIT, collective_id=0, has_side_effects=True),
         name='latent_all',
-    )(num, stats, latents, norm_lat, enc_wkv, enc_wo, enc_mlp, wqkv, lwo, lw1, lw2)
-
-
-def decoder_kernel(q_ref, zn_ref, nq_ref, nm_ref, wq_ref, wkv_ref, wo_ref, mlp_ref, wout_ref, y_ref, kq_s, vo_s, xu_s, u_s, p_s):
-    b = pl.program_id(0)
-    nb, n, dim = zn_ref.shape
-
-    @pl.when(b == 0)
-    def _():
-        def prepare(k, carry):
-            zn = zn_ref[pl.ds(k * 4, 4)].reshape(4 * n, dim)
-            high, low = split_bf16(dot_t(dot(zn, wkv_ref[0]).astype(BF16), wq_ref[...]))
-            kq_s[pl.ds(k * 4, 4), 0:n, :] = high.reshape(4, n, dim)
-            kq_s[pl.ds(k * 4, 4), n:2 * n, :] = low.reshape(4, n, dim)
-            high, low = split_bf16(dot(dot(zn, wkv_ref[1]).astype(BF16), wo_ref[...]))
-            vo_s[pl.ds(k * 4, 4), 0:n, :] = high.reshape(4, n, dim)
-            vo_s[pl.ds(k * 4, 4), n:2 * n, :] = low.reshape(4, n, dim)
-            return carry
-
-        lax.fori_loop(0, nb // 4, prepare, 0)
-        xu_s[...] = jnp.zeros_like(xu_s)
-        u_s[...] = jnp.zeros_like(u_s)
-
-    ahead = lax.rem(b, 2)
-    now = 1 - ahead
-    seq = jnp.minimum(b, nb - 1)
-    rows = q_ref.shape[1]
-    nblk = rows // RBLK
-    cblk = dim // nblk
-    xu = xu_s[now]
-    hidden = []
-    for k in range(nblk):
-        part = pl.ds(k * RBLK, RBLK)
-        cols = slice(k * cblk, (k + 1) * cblk)
-        hidden.append(gelu(dot(xu, mlp_ref[0, :, cols])).astype(BF16))
-        xq = layer_norm(q_ref[0, part].astype(F32), nq_ref[0:1, :], nq_ref[1:2, :])
-        both = dot_t(xq, kq_s[seq])
-        scores = (both + pltpu.roll(both, n, 1)) * (1.0 / math.sqrt(dim))
-        weights = jnp.exp(scores - jnp.max(scores, axis=1, keepdims=True))
-        probs = (weights / (0.5 * jnp.sum(weights, axis=1, keepdims=True))).astype(BF16)
-        p_s[part] = probs
-    hidden = jnp.concatenate(hidden, axis=1)
-    out = []
-    for k in range(nblk):
-        part = pl.ds(k * RBLK, RBLK)
-        cols = slice(k * cblk, (k + 1) * cblk)
-        out.append((u_s[now, :, cols] + dot(hidden, mlp_ref[1, :, cols])).astype(BF16))
-        u = dot(p_s[part], vo_s[seq])
-        u_s[ahead, part] = u
-        xu_s[ahead, part] = layer_norm(u, nm_ref[0:1, :], nm_ref[1:2, :])
-    out = jnp.concatenate(out, axis=1)
-    y_ref[0] = dot(out, wout_ref[...])
-
-
-def decoder(q_loc, zn, norm_query, norm_mlp, dec_wq, dec_wkv, dec_wo, dec_mlp, dec_out):
-    nb, rows, dim = q_loc.shape
-    n = zn.shape[1]
-    whole = lambda shape: pl.BlockSpec(shape, lambda b: (0,) * len(shape), pipeline_mode=pl.Buffered(1))
+    )(num, stats, latents, norm_lat, norm_query, enc_wkv, enc_wo, enc_mlp, wqkv, lwo, lw1, lw2,
+      q_loc, dec_wq, dec_wkv, dec_wo, dec_mlp)
+
+
+def out_kernel(u_ref, w_ref, y_ref):
+    for j in range(u_ref.shape[0]):
+        y_ref[j] = dot(u_ref[j], w_ref[...])
+
+
+def out_product(u, dec_out):
+    nb, rows, dim = u.shape
     return pl.pallas_call(
-        decoder_kernel,
-        grid=(nb + 1,),
-        in_specs=[pl.BlockSpec((1, rows, dim), lambda b: (jnp.minimum(b, nb - 1), 0, 0)), whole(zn.shape), whole((2, dim)), whole((2, dim)),
-                  whole((dim, dim)), whole((2, dim, dim)), whole((dim, dim)), whole((2, dim, dim)), whole((dim, dim))],
-        out_specs=pl.BlockSpec((1, rows, dim), lambda b: (jnp.maximum(b - 1, 0), 0, 0)),
+        out_kernel,
+        grid=(nb // OUT_STEP,),
+        in_specs=[pl.BlockSpec((OUT_STEP, rows, dim), lambda b: (b, 0, 0)), pl.BlockSpec((dim, dim), lambda b: (0, 0))],
+        out_specs=pl.BlockSpec((OUT_STEP, rows, dim), lambda b: (b, 0, 0)),
         out_shape=jax.ShapeDtypeStruct((nb, rows, dim), F32),
-        scratch_shapes=[pltpu.VMEM((nb, 2 * n, dim), BF16), pltpu.VMEM((nb, 2 * n, dim), BF16),
-                        pltpu.VMEM((2, rows, dim), BF16), pltpu.VMEM((2, rows, dim), F32), pltpu.VMEM((rows, LANES), BF16)],
         compiler_params=pltpu.CompilerParams(vmem_limit_bytes=VMEM_LIMIT),
-        name='dec_local',
-    )(q_loc, zn, norm_query, norm_mlp, dec_wq, dec_wkv, dec_wo, dec_mlp, dec_out)
+        name='out_product',
+    )(u, dec_out)
 
 
 def solution(mesh):
@@ -641,7 +696,8 @@
         wqkv = lat_wqkv.transpose(0, 2, 3, 1, 4)
         lwo = lat_wo.reshape(layers, -1, dim)
         num, stats = encoder_local(x_loc, norm_in, latents, norm_lat[0], enc_wq, enc_wkv)
-        zn = latent_all(num, stats, latents, norm_lat, enc_wkv, enc_wo, enc_mlp, wqkv, lwo, lat_w1, lat_w2)
-        return decoder(q_loc, zn, norm_query, norm_lat[7], dec_wq, dec_wkv, dec_wo, dec_mlp, dec_out)
+        u = latent_all(num, stats, q_loc, latents, norm_lat, norm_query, enc_wkv, enc_wo, enc_mlp, wqkv, lwo, lat_w1, lat_w2,
+                       dec_wq, dec_wkv, dec_wo, dec_mlp)
+        return out_product(u, dec_out)
 
     return jax.shard_map(device_step, mesh=mesh, in_specs=in_specs, out_specs=seq_spec, check_vma=False)

time: 257 us -> 239 us (0.930)
  Pallas kernels: 251 us -> 233 us
    pallas_call x2, Pallas kernels: 237 us -> 220 us  [the longest x1 204 us: latent_all(): pl.pallas_call(latent_kernel, in_specs=[vm] * 5 + [hbm] * 12, out_specs=h...]
where the time goes in v3:
time: 239 us
  Pallas kernels  233 us (97%)
  local copies, waits for them, and re-layouts  5.45 us (2%)
    pallas_call x1, Pallas kernels, latent_all(): pl.pallas_call(latent_kernel, in_specs=[vm] * 5 + [hbm] * 12, out_specs=h...  204 us
    pallas_call x1, Pallas kernels, out_product(): pl.pallas_call(out_kernel, grid=(nb // OUT_STEP,), in_specs=[pl.BlockSpec...  15.8 us
    pallas_call x1, Pallas kernels, encoder_local(): pl.pallas_call(encoder_kernel, grid=(nb // ENC_STEP,), in_specs=[pl.Block...  13.4 us

profile of v3, /device:TPU:0, one launch (start us, length us, event | category | flops | bytes accessed | tf_op | source)
XLA Modules:
  0.0 238.6 jit_solution(11876739258767740730)
XLA Ops:
  0.0 1.3 slice_bitcast_fusion.nq_ref
  1.3 4.2 %copy.22 = bf16[2,1024,3,2,128]{4,1,3,2,0:T(8,128)(2,1)} copy(bf16[2,1024,3,2,128]{4,3,2,1,0:T(2,128)(2,1)} %param.29) | data formatting | bytes 6291456 | tf_op args[10]
  5.5 13.4 %enc_local.1 = (f32[16,64,1024]{2,1,0:T(8,128)}, f32[16,128]{1,0:T(8,128)}) custom-call(bf16[16,256,1024]{2,1,0:T(8,128)(2,1)} %x_ref.1, f32[2,1024]{1,0:T(2,128)} %nin_ref.1, bf16[64,1024]{1,0:T(8,128)(2,1)} %lat_ref.3, f32[2,1024]{1,0:T(2,128)} %slice_bitcast_fusion.nq_ref, bf16[1024,1024]{1,0:T(8,128)(2,1)} %wq_ref.1, bf16[2,1024,1024]{2,1,0:T(8,128)(2,1)} %wkv_h.1), custom_call_target="tpu_custom_call" | custom-call | tf_op jit(solution)/shard_map/enc_local/pallas_call | solution.py:82
  18.9 203.9 %latent_all.1.u_ref = bf16[16,256,1024]{2,1,0:T(8,128)(2,1)} custom-call(f32[16,64,1024]{2,1,0:T(8,128)} %get-tuple-element.7.num_ref, f32[16,128]{1,0:T(8,128)} %get-tuple-element.8.st_ref, bf16[64,1024]{1,0:T(8,128)(2,1)} %lat_ref.3, f32[8,2,1024]{2,1,0:T(2,128)} %nlat_ref.1, f32[2,1024]{1,0:T(2,128)} %nq_ref.1, bf16[2,1024,1024]{2,1,0:T(8,128)(2,1)} %wkv_h.1, ...), custom_call_target="tpu_custom_call" | custom-call | tf_op jit(solution)/shard_map/latent_all/pallas_call | solution.py:645
  222.8 15.8 %out_product.1 = f32[16,256,1024]{2,1,0:T(8,128)} custom-call(bf16[16,256,1024]{2,1,0:T(8,128)(2,1)} %latent_all.1.u_ref, bf16[1024,1024]{1,0:T(8,128)(2,1)} %w_ref.1), custom_call_target="tpu_custom_call" | custom-call | tf_op jit(solution)/shard_map/out_product/pallas_call | solution.py:675

commit v4 on v1

v4 whole, which is shorter than its diff:
```python
import functools
import math
import jax
import jax.numpy as jnp
from jax import lax
from jax.experimental import pallas as pl
from jax.experimental.pallas import tpu as pltpu
from jax.sharding import PartitionSpec as P

LN_EPS = 1e-5
F32, BF16 = jnp.float32, jnp.bfloat16
MESH = pl.DeviceIdType.MESH
VMEM_LIMIT = 63 * 1024 * 1024
LANES = 128
NLINE = 4
RBLK = 128
CBLK = 256
OUT_STEP = 4
PAIR_AT = 4
NCH = 4
GELU_C = math.sqrt(2.0 / math.pi)


def layer_norm(values, gain, bias):
    row_mean = jnp.mean(values, axis=-1, keepdims=True)
    centered = values - row_mean
    row_var = jnp.mean(centered * centered, axis=-1, keepdims=True)
    return (centered * lax.rsqrt(row_var + LN_EPS) * gain + bias).astype(BF16)


def gelu(x):
    return 0.5 * x * (1.0 + jnp.tanh(GELU_C * (x + 0.044715 * (x * x * x))))


def repeat(count, step):
    lax.fori_loop(0, count, step, 0)


def each_peer(step):
    lax.fori_loop(1, 16, step, 0)


def dot(a, b):
    return jnp.dot(a, b, preferred_element_type=F32)


def dot_t(a, b):
    return lax.dot_general(a, b, (((1,), (1,)), ((), ())), preferred_element_type=F32)


def split_bf16(x):
    high = x.astype(BF16)
    return high, (x - high.astype(F32)).astype(BF16)


def latent_kernel(nin_ref, lat_ref, nlat_ref, nq_ref, x_h, ewq_h, wkv_h, wo_h, emlp_h, qkv_h, lwo_h, lw1_h, lw2_h,
                  q_h, dwq_h, dwkv_h, dwo_h, dmlp_h, dout_h, out_h, p_h, voo_h, w2o_h,
                  wv, wo, emlp, wqkv, lwo, lw1, lw2, wsem, wkq, wvo, wvoo, w2o,
                  kq_s, vo_s, voo_s, xq_s, xu0, xu1, p0, p1, q0, q1, h0, h1, xbuf, qsem, usem, psem, vsem, xsem,
                  num, qk_s, stats_s, st_mine,
                  st_all, gs, d2d, ysend, yrecv, zsum, rz_a, rz_b, ln_n, ln_f, ac_n, ac_f, zown, zall,
                  s_st, r_st, s_d2, r_d2, s_y, r_y, s_za, s_zb, r_za, r_zb,
                  s_lnn, s_lnf, s_acn, s_acf, r_lnn, r_lnf, r_acn, r_acf, r_ag, s_agz, s_agc, s_agy):
    n, dim = lat_ref.shape
    rows = n // NCH
    x = lax.axis_index('dp')
    t = lax.axis_index('tp')
    sp = lax.axis_index('sp')
    y = lax.div(sp, 2)
    c = lax.rem(sp, 2)
    me = t * 4 + sp
    upper = lax.div(t, 2)
    is_end = jnp.logical_or(t == 0, t == NLINE - 1)
    is_mid = jnp.logical_not(is_end)
    e_near = upper
    e_far = 1 - upper
    inward = (x, jnp.where(t == 0, 1, jnp.where(t == 1, 2, jnp.where(t == 2, 1, 2))), sp)
    outward = (x, jnp.where(t <= 1, 0, NLINE - 1), sp)
    core_peer = (x, t, y * 2 + (1 - c))
    y_peer = (x, t, (1 - y) * 2 + c)

    def rc(src, dst, ssem, rsem, dev):
        return pltpu.make_async_remote_copy(src_ref=src, dst_ref=dst, send_sem=ssem, recv_sem=rsem,
                                            device_id=dev, device_id_type=MESH)

    def peer(p):
        g = lax.rem(me + p, 16)
        return g, (x, lax.div(g, 4), lax.rem(g, 4))

    def fetch(first, pairs):
        copies = [pltpu.make_async_copy(src, dst, wsem.at[first + k]) for k, (src, dst) in enumerate(pairs)]
        for copy in copies:
            copy.start()
        return copies

    def x_copy(g):
        first, _, _ = group(g)
        slot = lax.rem(g, 2)
        return pltpu.make_async_copy(x_h.at[pl.ds(first, 2)], xbuf.at[pl.ds(2 * slot, 2)], xsem.at[slot])

    def group(g):
        i = lax.div(g, 4)
        j = lax.rem(g, 4)
        core = lax.div(j, 2)
        cb = 1 - c + core * (2 * c - 1)
        side = lax.rem(j, 2)
        yb = 1 - y + side * (2 * y - 1)
        return yb * 8 + cb * 4 + i * 2, i, j

    query_loads = fetch(0, ((ewq_h, wv), (wkv_h.at[0], wo)))
    x_copy(0).start()
    key_loads = fetch(2, ((dwkv_h, emlp),))
    lat_loads = fetch(3, ((qkv_h, wqkv), (lwo_h, lwo), (lw1_h, lw1)))
    out_loads = fetch(13, ((dmlp_h.at[1], lw2.at[0]), (dout_h, lw2.at[1])))

    barrier = pltpu.get_barrier_semaphore()

    def greet(p, carry):
        pl.semaphore_signal(barrier, inc=1, device_id=peer(p)[1], device_id_type=MESH)
        return carry

    each_peer(greet)

    def norm(index, values):
        return layer_norm(values, nlat_ref[index, 0:1, :], nlat_ref[index, 1:2, :])

    for load in query_loads:
        load.wait()
    q = dot(norm(0, lat_ref[...].astype(F32)), wv[...]).astype(BF16)
    high, low = split_bf16(dot_t(q, wo[...]))
    qk_s[0:n, :] = high
    qk_s[n:2 * n, :] = low
    stats_s[...] = jnp.zeros_like(stats_s)
    dec_loads = key_loads + fetch(11, ((dwq_h, wv), (dwo_h, wo)))

    def core_copy(i, yb):
        return rc(num.at[pl.ds(yb * 8 + (1 - c) * 4 + i * 2, 2)], d2d.at[i, yb], s_d2.at[i, yb], r_d2.at[i, yb], core_peer)

    def y_copy(i, e):
        return rc(ysend.at[i, e], yrecv.at[i, e], s_y.at[i, e], r_y.at[i, e], y_peer)

    def stats_copy(i, src, g, dev):
        return rc(st_mine.at[i], st_all.at[i, src], s_st.at[i, g], r_st.at[i, src], dev)

    lane = lax.broadcasted_iota(jnp.int32, (2 * n, LANES), 1)

    partner = t * 4 + y * 2 + (1 - c)

    def set_scales(first, second):
        gs[...] = jnp.zeros_like(gs)
        gs[0:16, :] = first
        upper_part = gs[...].T[0:n, :]
        gs[0:16, :] = second
        lower_part = gs[...].T[0:n, :]
        gs[0:n, :] = upper_part
        gs[n:2 * n, :] = lower_part

    def scales(b):
        col = jnp.sum(jnp.where(lane == b, gs[...], 0.0), axis=1, keepdims=True)
        return col[0:n], col[n:2 * n]

    def pair_step(i):
        stats_copy(i, partner, partner, core_peer).wait_recv()
        mine, other = st_all[i, me], st_all[i, partner]
        top = jnp.maximum(mine, other)
        set_scales(jnp.exp(mine - top), jnp.exp(other - top))
        for side in range(2):
            yb = y if side else 1 - y
            core_copy(i, yb).wait_recv()
            for e in range(2):
                b = yb * 8 + c * 4 + i * 2 + e
                first, second = scales(b)
                value = first * num[b] + second * d2d[i, yb, e]
                if side:
                    zsum[i, e] = value
                else:
                    ysend[i, e] = value
                    y_copy(i, e).start()

    def encode(g, carry):
        first, i, j = group(g)
        x_copy(g).wait()

        @pl.when(g < 7)
        def _():
            x_copy(g + 1).start()

        slot = 2 * lax.rem(g, 2)
        each = range(2)
        xns = [layer_norm(xbuf[slot + k].astype(F32), nin_ref[0:1, :], nin_ref[1:2, :]) for k in each]
        both = [dot_t(qk_s[...], xn) for xn in xns]
        scores = [(v[:n] + v[n:]) * (1.0 / math.sqrt(dim)) for v in both]
        maxima = [jnp.max(v, axis=1, keepdims=True) for v in scores]
        weights = [jnp.exp(v - m) for v, m in zip(scores, maxima)]
        sums = [jnp.sum(v, axis=1, keepdims=True) for v in weights]
        for k in each:
            num[first + k] = dot(weights[k].astype(BF16), xns[k])
            here = lax.broadcasted_iota(jnp.int32, (n, LANES), 1) == first + k
            stats_s[0:n, :] = jnp.where(here, maxima[k], stats_s[0:n, :])
            stats_s[n:2 * n, :] = jnp.where(here, sums[k], stats_s[n:2 * n, :])

        @pl.when(j == 1)
        def _():
            core_copy(i, 1 - y).start()
            core_copy(i, y).start()

        @pl.when(j == 3)
        def _():
            mine = stats_s[...].T[0:16, :]
            st_mine[i] = mine
            st_all[i, me] = mine

            def send_stats(p, inner):
                dst, dev = peer(p)
                stats_copy(i, me, dst, dev).start()
                return inner

            each_peer(send_stats)

        @pl.when(g == PAIR_AT)
        def _():
            pair_step(0)

        return carry

    pl.semaphore_wait(barrier, 15)
    repeat(8, encode)

    def y_add(i):
        def wait_stats(p, carry):
            g, dev = peer(p)

            @pl.when(g != partner)
            def _():
                stats_copy(i, g, g, dev).wait_recv()

            return carry

        each_peer(wait_stats)
        top = lax.fori_loop(1, 16, lambda d, m: jnp.maximum(m, st_all[i, d]), st_all[i, 0])

        def add_sum(d, total):
            stats = st_all[i, d]
            return total + jnp.exp(stats - top) * pltpu.roll(stats, n, 1)

        total = lax.fori_loop(0, 16, add_sum, jnp.zeros_like(top))
        across = t * 4 + (1 - y) * 2
        here = jnp.maximum(st_all[i, me], st_all[i, partner])
        there = jnp.maximum(st_all[i, across], st_all[i, across + 1])
        set_scales(jnp.exp(here - top) / total, jnp.exp(there - top) / total)
        for e in range(2):
            first, second = scales(y * 8 + c * 4 + i * 2 + e)
            y_copy(i, e).wait_recv()
            zsum[i, e] = first * zsum[i, e] + second * yrecv[i, e]

    def chunk(ch):
        return pl.ds(pl.multiple_of(ch * rows, rows), rows)

    def z_end_send(i):
        def step(ch, carry):
            rc(zsum.at[i, e_far, chunk(ch)], rz_a.at[i, chunk(ch)], s_za.at[i, ch], r_za.at[i, ch], inward).start()
            return carry
        repeat(NCH, step)

    def z_mid(i):
        def near(ch, carry):
            cp = rc(rz_a.at[i, chunk(ch)], rz_b.at[i, chunk(ch)], s_za.at[i, ch], r_zb.at[i, ch], inward)
            rc(rz_a.at[i, chunk(ch)], rz_a.at[i, chunk(ch)], s_za.at[i, ch], r_za.at[i, ch], outward).wait_recv()
            rz_a[i, chunk(ch)] = rz_a[i, chunk(ch)] + zsum[i, e_far, chunk(ch)]
            cp.start()
            return carry

        def far(ch, carry):
            cp = rc(rz_b.at[i, chunk(ch)], rz_b.at[i, chunk(ch)], s_zb.at[i, ch], r_zb.at[i, ch], outward)
            cp.wait_recv()
            rz_b[i, chunk(ch)] = rz_b[i, chunk(ch)] + zsum[i, e_near, chunk(ch)]
            cp.start()
            return carry

        repeat(NCH, near)
        repeat(NCH, far)

    def z_end_recv(i):
        def step(ch, carry):
            rc(rz_b.at[i, chunk(ch)], rz_b.at[i, chunk(ch)], s_zb.at[i, ch], r_zb.at[i, ch], inward).wait_recv()
            return carry
        repeat(NCH, step)
        return rz_b[i] + zsum[i, e_near]

    def attention(layer, xn):
        hd = wqkv.shape[4]
        qkv = [dot(xn, jnp.concatenate([wqkv[layer, j, 0], wqkv[layer, j, 1]], axis=1)).astype(BF16) for j in range(3)]
        outs = []
        for h in range(2):
            q, k, v = (part[:, h * hd:(h + 1) * hd] for part in qkv)
            scores = dot_t(q, k) * (1.0 / math.sqrt(hd))
            weights = jnp.exp(scores - jnp.max(scores, axis=1, keepdims=True))
            probs = (weights / jnp.sum(weights, axis=1, keepdims=True)).astype(BF16)
            outs.append(dot(probs, v).astype(BF16))
        return dot(jnp.concatenate(outs, axis=1), lwo[layer])

    def mlp(layer, xn):
        return dot(gelu(dot(xn, lw1[layer])).astype(BF16), lw2[layer])

    kinds = (attention, mlp)

    def ln_near(u, ch):
        return ln_n.at[u, chunk(ch)]

    def source(kind, layer, u, s):
        values = zown[s]
        xn = norm(2 + 2 * layer + kind, values)
        ln_n[u] = xn.astype(F32)

        def send_ln(ch, carry):
            rc(ln_n.at[u, chunk(ch)], ln_n.at[u, chunk(ch)], s_lnn.at[u, ch], r_lnn.at[u, ch], inward).start()
            return carry

        repeat(NCH, send_ln)
        ac_n[u] = values + kinds[kind](layer, xn)

        def send_ac(ch, carry):
            rc(ac_n.at[u, chunk(ch)], ac_n.at[u, chunk(ch)], s_acn.at[u, ch], r_acn.at[u, ch], inward).start()
            return carry

        repeat(NCH, send_ac)

    def sink(kind, layer, u, s):
        def wait_ln(ch, carry):
            rc(ln_f.at[u, chunk(ch)], ln_f.at[u, chunk(ch)], s_lnf.at[u, ch], r_lnf.at[u, ch], inward).wait_recv()
            return carry

        repeat(NCH, wait_ln)
        part = kinds[kind](layer, ln_f[u].astype(BF16))

        def wait_ac(ch, carry):
            rc(ac_f.at[u, chunk(ch)], ac_f.at[u, chunk(ch)], s_acf.at[u, ch], r_acf.at[u, ch], inward).wait_recv()
            return carry

        repeat(NCH, wait_ac)
        zown[s] = ac_f[u] + part

    def middle(kind, layer, u):
        def near_ln(ch, carry):
            rc(ln_n.at[u, chunk(ch)], ln_n.at[u, chunk(ch)], s_lnn.at[u, ch], r_lnn.at[u, ch], outward).wait_recv()
            rc(ln_n.at[u, chunk(ch)], ln_f.at[u, chunk(ch)], s_lnn.at[u, ch], r_lnf.at[u, ch], inward).start()
            return carry

        repeat(NCH, near_ln)
        zown[0] = kinds[kind](layer, ln_n[u].astype(BF16))

        def both(ch, carry):
            cp = rc(ln_f.at[u, chunk(ch)], ln_f.at[u, chunk(ch)], s_lnf.at[u, ch], r_lnf.at[u, ch], outward)
            cp.wait_recv()
            cp.start()
            rc(ac_n.at[u, chunk(ch)], ac_n.at[u, chunk(ch)], s_acn.at[u, ch], r_acn.at[u, ch], outward).wait_recv()
            ac_n[u, chunk(ch)] = ac_n[u, chunk(ch)] + zown[0, chunk(ch)]
            rc(ac_n.at[u, chunk(ch)], ac_f.at[u, chunk(ch)], s_acn.at[u, ch], r_acf.at[u, ch], inward).start()
            return carry

        repeat(NCH, both)
        zown[1] = kinds[kind](layer, ln_f[u].astype(BF16))
        if kind == 1:
            @pl.when(u == 7)
            def _():
                ag_relay(0, e_near, inward)

        def far_ac(ch, carry):
            cp = rc(ac_f.at[u, chunk(ch)], ac_f.at[u, chunk(ch)], s_acf.at[u, ch], r_acf.at[u, ch], outward)
            cp.wait_recv()
            ac_f[u, chunk(ch)] = ac_f[u, chunk(ch)] + zown[1, chunk(ch)]
            cp.start()
            return carry

        repeat(NCH, far_ac)

    def line_seq(i, e):
        return y * 8 + c * 4 + i * 2 + e

    def ag_copy(b, ch, sems, dev):
        return rc(zall.at[b, chunk(ch)], zall.at[b, chunk(ch)], sems.at[b, ch], r_ag.at[b, ch], dev)

    def ag_send(b, ch, z_dev):
        if z_dev is not None:
            ag_copy(b, ch, s_agz, z_dev).start()
        ag_copy(b, ch, s_agy, y_peer).start()
        ag_copy(b, ch, s_agc, core_peer).start()

    def ag_source(i):
        b = line_seq(i, e_near)
        zall[b] = norm(6, zown[i]).astype(F32)

        def step(ch, carry):
            ag_send(b, ch, inward)
            return carry

        repeat(NCH, step)

    def ag_relay(i, e, z_dev):
        b = line_seq(i, e)

        def step(ch, carry):
            ag_copy(b, ch, s_agz, inward).wait_recv()
            ag_send(b, ch, z_dev)
            return carry

        repeat(NCH, step)

    def ag_cross(i, e):
        b = (1 - y) * 8 + c * 4 + i * 2 + e

        def step(ch, carry):
            ag_copy(b, ch, s_agy, y_peer).wait_recv()
            ag_copy(b, ch, s_agc, core_peer).start()
            return carry

        repeat(NCH, step)

    for load in dec_loads:
        load.wait()

    def products(k, carry):
        part = pl.ds(pl.multiple_of(k * 256, 256), 256)
        wkq[part] = dot_t(emlp[0, part], wv[...]).astype(BF16)
        wvo[part] = dot(emlp[1, part], wo[...]).astype(BF16)
        return carry

    repeat(dim // 256, products)
    enc_loads = fetch(7, ((wkv_h.at[1], wv), (wo_h, wo), (emlp_h, emlp)))
    pair_step(1)
    for load in out_loads:
        load.wait()

    def out_products(k, carry):
        part = pl.ds(pl.multiple_of(k * 256, 256), 256)
        w2o[part] = dot(lw2[0, part], lw2[1]).astype(BF16)
        wvoo[part] = dot(wvo[part], lw2[1]).astype(BF16)
        return carry

    repeat(dim // 256, out_products)
    lat_loads = lat_loads + fetch(6, ((lw2_h, lw2),))
    w2o_copy = pltpu.make_async_copy(w2o, w2o_h, wsem.at[15])
    w2o_copy.start()
    def tail_loads():
        return [pltpu.make_async_copy(dmlp_h.at[0], emlp.at[0], wsem.at[10])]

    def order(k):
        i = lax.div(k, 8)
        r = lax.rem(k, 8)
        pair = lax.div(r, 2)
        odd = lax.rem(pair, 2)
        yb = y + odd - 2 * y * odd
        core = lax.rem(r, 2)
        cb = c + core - 2 * c * core
        far = lax.div(pair, 2)
        e = e_near + far - 2 * e_near * far
        return yb * 8 + cb * 4 + i * 2 + e

    def q_copy(k, par):
        return pltpu.make_async_copy(q_h.at[order(k)], (q0, q1)[par], qsem.at[par])

    def u_copy(k, par):
        return pltpu.make_async_copy((h0, h1)[par], out_h.at[order(k)], usem.at[par])

    def p_copy(k, par):
        return pltpu.make_async_copy((p0, p1)[par], p_h.at[order(k)], psem.at[par])

    def voo_copy(k, par):
        return pltpu.make_async_copy(voo_s.at[par], voo_h.at[order(k)], vsem.at[par])

    nrow = q0.shape[0]

    def decode_start():
        q_copy(0, 0).start()
        q_copy(1, 1).start()
        for load in tail_loads():
            load.wait()

    def prepare(k):
        zn = jnp.concatenate([zall[order(k)], zall[order(k + 1)]], axis=0).astype(BF16)

        def piece(weights, target):
            high, low = split_bf16(dot(zn, weights[...]))
            for j in range(2):
                target[j, 0:n, :] = high[j * n:(j + 1) * n]
                target[j, n:2 * n, :] = low[j * n:(j + 1) * n]

        return [functools.partial(piece, *pair) for pair in ((wkq, kq_s), (wvo, vo_s), (wvoo, voo_s))]

    parts = [slice(r, r + RBLK) for r in range(0, nrow, RBLK)]

    def norm_q(par):
        def piece(part):
            xq_s[part] = layer_norm((q0, q1)[par][part].astype(F32), nq_ref[0:1, :], nq_ref[1:2, :])

        return [functools.partial(piece, part) for part in parts]

    def score(par):
        def piece(part):
            both = dot_t(xq_s[part], kq_s[par])
            scores = (both + pltpu.roll(both, n, 1)) * (1.0 / math.sqrt(dim))
            weights = jnp.exp(scores - jnp.max(scores, axis=1, keepdims=True))
            (p0, p1)[par][part] = (weights / (0.5 * jnp.sum(weights, axis=1, keepdims=True))).astype(BF16)

        return [functools.partial(piece, part) for part in parts]

    def attend(par):
        def piece(part):
            (xu0, xu1)[par][part] = norm(7, dot((p0, p1)[par][part], vo_s[par]))

        return [functools.partial(piece, part) for part in parts]

    def expand(par):
        def piece(col):
            cols = slice(col, col + CBLK)
            (h0, h1)[par][:, cols] = gelu(dot((xu0, xu1)[par][...], emlp[0, :, cols])).astype(BF16)

        return [functools.partial(piece, col) for col in range(0, dim, CBLK)]

    def emit(*lists):
        for k in range(max(len(pieces) for pieces in lists)):
            for pieces in lists:
                if k < len(pieces):
                    pieces[k]()

    def decode_pair(kk, first):
        k = 2 * kk

        def step(ch, inner):
            ag_copy(order(k + 1), ch, s_agc, core_peer).wait_recv()
            return inner

        repeat(NCH, step)
        if not first:
            for par in range(2):
                voo_copy(k - 2 + par, par).wait()
            p_copy(k - 2, 0).wait()

            @pl.when(kk >= 2)
            def _():
                u_copy(k - 3, 1).wait()

        q_copy(k, 0).wait()
        emit(prepare(k), norm_q(0))
        emit([] if first else expand(1), score(0) + attend(0))
        for par in range(2):
            voo_copy(k + par, par).start()
        p_copy(k, 0).start()
        if not first:
            u_copy(k - 1, 1).start()

        @pl.when(kk < 7)
        def _():
            q_copy(k + 2, 0).start()

        q_copy(k + 1, 1).wait()
        if not first:
            u_copy(k - 2, 0).wait()
            p_copy(k - 1, 1).wait()
        emit(norm_q(1)[:1])
        emit(expand(0), norm_q(1)[1:] + score(1) + attend(1))
        p_copy(k + 1, 1).start()
        u_copy(k, 0).start()

        @pl.when(kk < 7)
        def _():
            q_copy(k + 3, 1).start()

    def decode_end():
        for par in range(2):
            voo_copy(14 + par, par).wait()
            p_copy(14 + par, par).wait()
        u_copy(13, 1).wait()
        emit(expand(1))
        u_copy(15, 1).start()
        u_copy(14, 0).wait()
        u_copy(15, 1).wait()
        w2o_copy.wait()

    def relays(kk):
        def far_relay(i):
            @pl.when(jnp.logical_and(is_mid, kk == (1, 3)[i]))
            def _():
                ag_relay(i, e_far, outward)

            @pl.when(jnp.logical_and(is_end, kk == (2, 5)[i]))
            def _():
                ag_relay(i, e_far, None)

        def near_relay(i):
            @pl.when(is_mid)
            def _():
                ag_relay(i, e_near, inward)

        pl.when(kk == 1)(lambda: ag_cross(0, e_near))
        far_relay(0)
        pl.when(kk == 2)(lambda: near_relay(1))
        pl.when(kk == 3)(lambda: ag_cross(0, e_far))
        far_relay(1)
        pl.when(kk == 4)(lambda: ag_cross(1, e_near))
        pl.when(kk == 6)(lambda: ag_cross(1, e_far))

    y_add(0)

    @pl.when(is_end)
    def _():
        z_end_send(0)

    @pl.when(is_mid)
    def _():
        z_mid(0)

    y_add(1)
    for load in lat_loads + enc_loads:
        load.wait()

    @pl.when(is_end)
    def _():
        z_end_send(1)

        def start(s, carry):
            both = jnp.concatenate(split_bf16(z_end_recv(s)), axis=0)
            both = dot(both, wv[...])
            attended = (both[0:n] + both[n:2 * n]).astype(BF16)
            z = lat_ref[...].astype(F32) + dot(attended, wo[...])
            zown[s] = z + dot(gelu(dot(norm(1, z), emlp[0])).astype(BF16), emlp[1])
            source(0, 0, s, s)
            return carry

        repeat(2, start)
        for load in tail_loads():
            load.start()

        def layer_step(layer, carry):
            def attn_unit(s, inner):
                u = layer * 4 + s
                sink(0, layer, u, s)
                source(1, layer, u + 2, s)
                return inner

            repeat(2, attn_unit)

            def mlp_unit(s, inner):
                u = layer * 4 + 2 + s

                @pl.when(u == 7)
                def _():
                    decode_start()
                    decode_pair(0, True)

                sink(1, layer, u, s)

                @pl.when(layer == 0)
                def _():
                    source(0, 1, u + 2, s)

                @pl.when(layer == 1)
                def _():
                    ag_source(s)

                return inner

            repeat(2, mlp_unit)
            return carry

        repeat(2, layer_step)

    @pl.when(is_mid)
    def _():
        z_mid(1)
        for load in tail_loads():
            load.start()

        def layer_step(layer, carry):
            for kind in range(2):
                def unit(s, inner):
                    middle(kind, layer, layer * 4 + 2 * kind + s)
                    return inner
                repeat(2, unit)
            return carry

        repeat(2, layer_step)

    @pl.when(is_mid)
    def _():
        decode_start()
        decode_pair(0, True)

    def tail_step(kk, carry):
        relays(kk)
        decode_pair(kk, False)
        return carry

    lax.fori_loop(1, 8, tail_step, 0)
    decode_end()

    def done_stats(p, carry):
        g, dev = peer(p)
        for i in range(2):
            stats_copy(i, me, g, dev).wait_send()
        return carry

    each_peer(done_stats)
    for i in range(2):
        core_copy(i, 1 - y).wait_send()
        core_copy(i, y).wait_send()
        for e in range(2):
            y_copy(i, e).wait_send()

    def done_z(i, carry):
        def step(ch, inner):
            rc(rz_a.at[i, chunk(ch)], rz_a.at[i, chunk(ch)], s_za.at[i, ch], r_za.at[i, ch], inward).wait_send()

            @pl.when(is_mid)
            def _():
                rc(rz_b.at[i, chunk(ch)], rz_b.at[i, chunk(ch)], s_zb.at[i, ch], r_zb.at[i, ch], outward).wait_send()

            return inner

        repeat(NCH, step)
        return carry

    repeat(2, done_z)

    def done_units(u, carry):
        def step(ch, inner):
            rc(ln_n.at[u, chunk(ch)], ln_n.at[u, chunk(ch)], s_lnn.at[u, ch], r_lnn.at[u, ch], inward).wait_send()
            rc(ac_n.at[u, chunk(ch)], ac_n.at[u, chunk(ch)], s_acn.at[u, ch], r_acn.at[u, ch], inward).wait_send()

            @pl.when(is_mid)
            def _():
                rc(ln_f.at[u, chunk(ch)], ln_f.at[u, chunk(ch)], s_lnf.at[u, ch], r_lnf.at[u, ch], outward).wait_send()
                rc(ac_f.at[u, chunk(ch)], ac_f.at[u, chunk(ch)], s_acf.at[u, ch], r_acf.at[u, ch], outward).wait_send()

            return inner

        repeat(NCH, step)
        return carry

    repeat(8, done_units)

    def done_ag(i, carry):
        for e in range(2):
            b = line_seq(i, e)
            other = (1 - y) * 8 + c * 4 + i * 2 + e

            def step(ch, inner):
                ag_copy(b, ch, s_agy, y_peer).wait_send()
                ag_copy(b, ch, s_agc, core_peer).wait_send()
                ag_copy(other, ch, s_agc, core_peer).wait_send()

                @pl.when(jnp.logical_or(is_mid, e == e_near))
                def _():
                    ag_copy(b, ch, s_agz, inward).wait_send()

                return inner

            repeat(NCH, step)
        return carry

    repeat(2, done_ag)


def latent_all(x_loc, q_loc, latents, norm_in, norm_lat, norm_query, enc_wq, enc_wkv, enc_wo, enc_mlp,
               wqkv, lwo, lw1, lw2, dec_wq, dec_wkv, dec_wo, dec_mlp, dec_out):
    nb, rows, dim = q_loc.shape
    n = latents.shape[0]
    vm = pl.BlockSpec(memory_space=pltpu.VMEM)
    hbm = pl.BlockSpec(memory_space=pl.ANY)
    dma = pltpu.SemaphoreType.DMA
    buf = lambda *shape: pltpu.VMEM(shape + (n, dim), F32)
    half = lambda *shape: pltpu.VMEM(shape + (dim,), BF16)
    return pl.pallas_call(
        latent_kernel,
        in_specs=[vm] * 4 + [hbm] * 15,
        out_specs=[hbm] * 4,
        out_shape=[jax.ShapeDtypeStruct(shape, BF16)
                   for shape in ((nb, rows, dim), (nb, rows, 2 * n), (nb, 2 * n, dim), (dim, dim))],
        scratch_shapes=[
            half(dim), half(dim), pltpu.VMEM(enc_mlp.shape, BF16),
            pltpu.VMEM(wqkv.shape, BF16), pltpu.VMEM(lwo.shape, BF16), pltpu.VMEM(lw1.shape, BF16), pltpu.VMEM(lw2.shape, BF16),
            dma((16,)), half(dim), half(dim), half(dim), half(dim),
            half(2, 2 * n), half(2, 2 * n), half(2, 2 * n), half(rows), half(rows), half(rows),
            pltpu.VMEM((rows, 2 * n), BF16), pltpu.VMEM((rows, 2 * n), BF16), half(rows), half(rows), half(rows), half(rows),
            half(4, rows), *[dma((2,))] * 5,
            buf(nb), half(2 * n), pltpu.VMEM((LANES, LANES), F32), pltpu.VMEM((2, nb, LANES), F32),
            pltpu.VMEM((2, 16, nb, LANES), F32), pltpu.VMEM((LANES, LANES), F32),
            buf(2, 2, 2), *[buf(2, 2)] * 3, *[buf(2)] * 2, *[buf(8)] * 4, buf(2), buf(nb),
            *[dma((2, 16))] * 2, *[dma((2, 2))] * 4, *[dma((2, NCH))] * 4,
        ] + [dma((8, NCH))] * 8 + [dma((nb, NCH))] * 4,
        compiler_params=pltpu.CompilerParams(vmem_limit_bytes=VMEM_LIMIT, collective_id=0, has_side_effects=True),
        name='latent_all',
    )(norm_in, latents, norm_lat, norm_query, x_loc, enc_wq, enc_wkv, enc_wo, enc_mlp, wqkv, lwo, lw1, lw2,
      q_loc, dec_wq, dec_wkv, dec_wo, dec_mlp, dec_out)


def out_kernel(h_ref, p_ref, voo_ref, w_ref, y_ref):
    for j in range(h_ref.shape[0]):
        y_ref[j] = dot(h_ref[j], w_ref[...]) + dot(p_ref[j], voo_ref[j])


def out_product(hidden, probs, voo, weights):
    nb, rows, dim = hidden.shape
    step = lambda *shape: pl.BlockSpec((OUT_STEP,) + shape, lambda b: (b, 0, 0))
    return pl.pallas_call(
        out_kernel,
        grid=(nb // OUT_STEP,),
        in_specs=[step(rows, dim), step(*probs.shape[1:]), step(*voo.shape[1:]), pl.BlockSpec((dim, dim), lambda b: (0, 0))],
        out_specs=step(rows, dim),
        out_shape=jax.ShapeDtypeStruct((nb, rows, dim), F32),
        compiler_params=pltpu.CompilerParams(vmem_limit_bytes=VMEM_LIMIT),
        name='out_product',
    )(hidden, probs, voo, weights)


def solution(mesh):
    seq_spec = P('dp', ('tp', 'sp'), None)
    replicated = P()
    in_specs = (seq_spec, seq_spec, replicated, replicated, replicated, replicated, replicated, replicated, replicated, replicated,
                P(None, None, None, 'tp', None), P(None, 'tp', None, None), P(None, None, 'tp'), P(None, 'tp', None),
                replicated, replicated, replicated, replicated, replicated)

    def device_step(x_loc, q_loc, latents, norm_in, norm_query, norm_lat, enc_wq, enc_wkv, enc_wo, enc_mlp,
                    lat_wqkv, lat_wo, lat_w1, lat_w2, dec_wq, dec_wkv, dec_wo, dec_mlp, dec_out):
        layers, dim = lat_wqkv.shape[0], latents.shape[1]
        wqkv = lat_wqkv.transpose(0, 2, 3, 1, 4)
        lwo = lat_wo.reshape(layers, -1, dim)
        parts = latent_all(x_loc, q_loc, latents, norm_in, norm_lat, norm_query, enc_wq, enc_wkv, enc_wo, enc_mlp,
                       wqkv, lwo, lat_w1, lat_w2, dec_wq, dec_wkv, dec_wo, dec_mlp, dec_out)
        return out_product(*parts)

    return jax.shard_map(device_step, mesh=mesh, in_specs=in_specs, out_specs=seq_spec, check_vma=False)
```

time: 282 us -> 223 us (0.79)
  Pallas kernels: 271 us -> 219 us
  local copies, waits for them, and re-layouts: 9.37 us -> 4.06 us
    pallas_call x3 -> x2, Pallas kernels: 271 us -> 219 us  [the longest x1 202 us: latent_all(): pl.pallas_call(latent_kernel, in_specs=[vm] * 4 + [hbm] * 15, out_specs=[...]
    reshape x1 -> x0, local copies, waits for them, and re-layouts: 8.04 us -> none  [device_step(): wqkv = lat_wqkv.reshape(layers, dim, -1)]
    unnamed x0 -> x1, local copies, waits for them, and re-layouts: none -> 4.06 us
where the time goes in v4:
time: 223 us
  Pallas kernels  219 us (98%)
  local copies, waits for them, and re-layouts  4.06 us (2%)
    pallas_call x1, Pallas kernels, latent_all(): pl.pallas_call(latent_kernel, in_specs=[vm] * 4 + [hbm] * 15, out_specs=[...  202 us
    pallas_call x1, Pallas kernels, out_product(): pl.pallas_call(out_kernel, grid=(nb // OUT_STEP,), in_specs=[step(rows, d...  16.9 us

profile of v4, /device:TPU:0, one launch (start us, length us, event | category | flops | bytes accessed | tf_op | source)
XLA Modules:
  0.0 223.1 jit_solution(12763234834959233668)
XLA Ops:
  0.0 4.1 %copy.22 = bf16[2,1024,3,2,128]{4,1,3,2,0:T(8,128)(2,1)} copy(bf16[2,1024,3,2,128]{4,3,2,1,0:T(2,128)(2,1)} %param.29) | data formatting | bytes 6291456 | tf_op args[10]
  4.1 202.1 %latent_all.1 = (bf16[16,256,1024]{2,1,0:T(8,128)(2,1)}, bf16[16,256,128]{2,1,0:T(8,128)(2,1)}, bf16[16,128,1024]{2,1,0:T(8,128)(2,1)}, bf16[1024,1024]{1,0:T(8,128)(2,1)}) custom-call(f32[2,1024]{1,0:T(2,128)} %nin_ref.1, bf16[64,1024]{1,0:T(8,128)(2,1)} %lat_ref.1, f32[8,2,1024]{2,1,0:T(2,128)} %nlat_ref.1, f32[2,1024]{1,0:T(2,128)} %nq_ref.1, ...), custom_call_target="tpu_custom_call" | custom-call | tf_op jit(solution)/shard_map/latent_all/pallas_call | solution.py:773
  206.2 16.9 %out_product.1 = f32[16,256,1024]{2,1,0:T(8,128)} custom-call(bf16[16,256,1024]{2,1,0:T(8,128)(2,1)} %get-tuple-element.9.h_ref, bf16[16,256,128]{2,1,0:T(8,128)(2,1)} %get-tuple-element.10.p_ref, bf16[16,128,1024]{2,1,0:T(8,128)(2,1)} %get-tuple-element.11.voo_ref, bf16[1024,1024]{1,0:T(8,128)(2,1)} %get-tuple-element.12.w_ref), custom_call_target="tpu_custom_call" | custom-call | tf_op jit(solution)/shard_map/out_product/pallas_call | solution.py:805

commit v5 on v4

--- a/solution.py
+++ b/solution.py
@@ -437,10 +437,8 @@
         wvoo[part] = dot(wvo[part], lw2[1]).astype(BF16)
         return carry
 
-    repeat(dim // 256, out_products)
-    lat_loads = lat_loads + fetch(6, ((lw2_h, lw2),))
-    w2o_copy = pltpu.make_async_copy(w2o, w2o_h, wsem.at[15])
-    w2o_copy.start()
+    halfway = dim // 512
+    repeat(halfway, out_products)
     def tail_loads():
         return [pltpu.make_async_copy(dmlp_h.at[0], emlp.at[0], wsem.at[10])]
 
@@ -605,6 +603,11 @@
     @pl.when(is_end)
     def _():
         z_end_send(0)
+
+    lax.fori_loop(halfway, 2 * halfway, out_products, 0)
+    lat_loads = lat_loads + fetch(6, ((lw2_h, lw2),))
+    w2o_copy = pltpu.make_async_copy(w2o, w2o_h, wsem.at[15])
+    w2o_copy.start()
 
     @pl.when(is_mid)
     def _():

time: 223 us -> 224 us (level)
  no operation moved by 1% of the time
where the time goes in v5:
time: 224 us; the launch traced here: 223 us
  Pallas kernels  219 us (98%)
  local copies, waits for them, and re-layouts  4.06 us (2%)
    pallas_call x1, Pallas kernels, latent_all(): pl.pallas_call(latent_kernel, in_specs=[vm] * 4 + [hbm] * 15, out_specs=[...  202 us
    pallas_call x1, Pallas kernels, out_product(): pl.pallas_call(out_kernel, grid=(nb // OUT_STEP,), in_specs=[step(rows, d...  16.9 us

profile of v5, /device:TPU:0, one launch (start us, length us, event | category | flops | bytes accessed | tf_op | source)
XLA Modules:
  0.0 223.2 jit_solution(15875963770755640740)
XLA Ops:
  0.0 4.1 %copy.22 = bf16[2,1024,3,2,128]{4,1,3,2,0:T(8,128)(2,1)} copy(bf16[2,1024,3,2,128]{4,3,2,1,0:T(2,128)(2,1)} %param.29) | data formatting | bytes 6291456 | tf_op args[10]
  4.1 202.2 %latent_all.1 = (bf16[16,256,1024]{2,1,0:T(8,128)(2,1)}, bf16[16,256,128]{2,1,0:T(8,128)(2,1)}, bf16[16,128,1024]{2,1,0:T(8,128)(2,1)}, bf16[1024,1024]{1,0:T(8,128)(2,1)}) custom-call(f32[2,1024]{1,0:T(2,128)} %nin_ref.1, bf16[64,1024]{1,0:T(8,128)(2,1)} %lat_ref.1, f32[8,2,1024]{2,1,0:T(2,128)} %nlat_ref.1, f32[2,1024]{1,0:T(2,128)} %nq_ref.1, ...), custom_call_target="tpu_custom_call" | custom-call | tf_op jit(solution)/shard_map/latent_all/pallas_call | solution.py:776
  206.3 16.9 %out_product.1 = f32[16,256,1024]{2,1,0:T(8,128)} custom-call(bf16[16,256,1024]{2,1,0:T(8,128)(2,1)} %get-tuple-element.9.h_ref, bf16[16,256,128]{2,1,0:T(8,128)(2,1)} %get-tuple-element.10.p_ref, bf16[16,128,1024]{2,1,0:T(8,128)(2,1)} %get-tuple-element.11.voo_ref, bf16[1024,1024]{1,0:T(8,128)(2,1)} %get-tuple-element.12.w_ref), custom_call_target="tpu_custom_call" | custom-call | tf_op jit(solution)/shard_map/out_product/pallas_call | solution.py:808
